TPU v7x, 32 devices: a whole 2x2x4 slice. The times are simulated.
32 devices in a mesh: dp: 8 (over y, x, core), tensor: 4 (over z).
Axes of the slice: x: 2, y: 2, z: 4, core: 2. Of those that a mesh axis runs over, the one named last changes fastest.
Arguments:
- tokens: bfloat16 [8192, 1280], P(('dp', 'tensor')), may hold values from -6 to 6
- w_query: bfloat16 [1280, 1280], P('dp', 'tensor'), may hold values from -0.15625 to 0.15625
- w_key: bfloat16 [1280, 1280], P('dp', 'tensor'), may hold values from -0.15625 to 0.15625
- w_value: bfloat16 [1280, 1280], P('dp', 'tensor'), may hold values from -0.15625 to 0.15625
- w_out: bfloat16 [1280, 1280], P('dp', 'tensor'), may hold values from -0.15625 to 0.15625
- w_up: bfloat16 [1280, 5120], P('dp', 'tensor'), may hold values from -0.15625 to 0.15625
- w_gate: bfloat16 [1280, 5120], P('dp', 'tensor'), may hold values from -0.15625 to 0.15625
- w_down: bfloat16 [1280, 5120], P('dp', 'tensor'), may hold values from -0.078125 to 0.078125
- qk_scale: float32 [1280], P('tensor'), may hold values from 0.8 to 1.8
- up_scale: float32 [5120], P('tensor'), may hold values from 0.5 to 2
- gate_scale: float32 [5120], P('tensor'), may hold values from 0.5 to 2
- alpha_attn: float32 [1280], replicated, may hold values from 0.2 to 0.6
- alpha_mlp: float32 [1280], replicated, may hold values from 0.2 to 0.6
- cotangent: bfloat16 [8192, 1280], P(('dp', 'tensor')), may hold values from -6 to 6
Outputs:
- output: bfloat16 [8192, 1280], P(('dp', 'tensor'))
- tokens_gradient: float32 [8192, 1280], P(('dp', 'tensor'))
- w_query_gradient: float32 [1280, 1280], P('dp', 'tensor')
- w_key_gradient: float32 [1280, 1280], P('dp', 'tensor')
- w_value_gradient: float32 [1280, 1280], P('dp', 'tensor')
- w_out_gradient: float32 [1280, 1280], P('dp', 'tensor')
- w_up_gradient: float32 [1280, 5120], P('dp', 'tensor')
- w_gate_gradient: float32 [1280, 5120], P('dp', 'tensor')
- w_down_gradient: float32 [1280, 5120], P('dp', 'tensor')
- qk_scale_gradient: float32 [1280], P('tensor')
- up_scale_gradient: float32 [5120], P('tensor')
- gate_scale_gradient: float32 [5120], P('tensor')
- alpha_attn_gradient: float32 [1280], replicated
- alpha_mlp_gradient: float32 [1280], replicated
All inputs are finite; a program needn't handle non-finite values.
Results may differ from a plain program's by a relative error of at most 0.017.
Values may be sent and summed in bfloat16 or wider, within the bound.
A program may use at most 192 MiB of HBM per device.

v0:
```python
import jax
import jax.numpy as jnp
from jax import lax
from jax.sharding import PartitionSpec as P

HEAD_DIM = 64


HIGH = lax.Precision.HIGHEST
EPS = 1e-06


def unit_rows(value):
    scale = lax.rsqrt(jnp.mean(value * value, axis=-1, keepdims=True) + EPS)
    return (value * scale, scale)


def unit_back(grad, unit, scale):
    return scale * (grad - unit * jnp.mean(grad * unit, axis=-1, keepdims=True))


def contract_rows(left, right):
    return lax.dot_general(
        left, right, (((0,), (0,)), ((), ())), preferred_element_type=jnp.float32
    )


def contract_cols(left, right):
    return lax.dot_general(
        left, right, (((1,), (1,)), ((), ())), preferred_element_type=jnp.float32
    )


def tables(width, length):
    half_dim = HEAD_DIM // 2
    column = lax.iota(jnp.int32, width)
    within = column % HEAD_DIM
    freq_index = (within % half_dim).astype(jnp.float32)
    frequency = 10000.0 ** (-freq_index / half_dim)
    position = lax.iota(jnp.float32, length)
    angle = position[:, None] * frequency[None, :]
    first_half = (within < half_dim)[None, :]
    heads = width // HEAD_DIM
    member = (
        lax.broadcasted_iota(jnp.int32, (width, heads), 0) // HEAD_DIM
        == lax.broadcasted_iota(jnp.int32, (width, heads), 1)
    ).astype(jnp.float32)
    return (jnp.cos(angle), jnp.sin(angle), first_half, member)


def rope_apply(value, cosine, sine, first_half):
    half_dim = HEAD_DIM // 2
    turned = jnp.where(
        first_half, -jnp.roll(value, -half_dim, axis=1), jnp.roll(value, half_dim, axis=1)
    )
    return value * cosine + turned * sine


def rope_back(grad, cosine, sine, first_half):
    half_dim = HEAD_DIM // 2
    weighted = grad * sine
    turned = jnp.where(
        first_half, jnp.roll(weighted, -half_dim, axis=1), -jnp.roll(weighted, half_dim, axis=1)
    )
    return grad * cosine + turned


def head_unit(value, member):
    mean_sq = (
        jnp.dot(value * value, member, precision=HIGH, preferred_element_type=jnp.float32)
        / HEAD_DIM
    )
    scale = jnp.dot(
        lax.rsqrt(mean_sq + EPS), member.T, precision=HIGH, preferred_element_type=jnp.float32
    )
    return (value * scale, scale)


def head_back(grad, unit, scale, member):
    inner = (
        jnp.dot(grad * unit, member, precision=HIGH, preferred_element_type=jnp.float32) / HEAD_DIM
    )
    spread = jnp.dot(inner, member.T, precision=HIGH, preferred_element_type=jnp.float32)
    return scale * (grad - unit * spread)


def block_scores(query3, key3, start, stop, block):
    scale = HEAD_DIM ** (-0.5)
    scores = (
        jnp.einsum(
            "qhd,khd->hqk", query3[start:stop], key3[:stop], preferred_element_type=jnp.float32
        )
        * scale
    )
    allowed = start + lax.broadcasted_iota(jnp.int32, (block, stop), 0) >= lax.broadcasted_iota(
        jnp.int32, (block, stop), 1
    )
    return jnp.where(allowed[None], scores, -jnp.inf)


def attend(query3, key3, value3, block):
    length = query3.shape[0]
    outputs = []
    totals = []
    for block_id in range(length // block):
        start = block_id * block
        stop = start + block
        scores = block_scores(query3, key3, start, stop, block)
        row_max = jnp.max(scores, axis=-1, keepdims=True)
        log_total = jnp.log(jnp.sum(jnp.exp(scores - row_max), axis=-1, keepdims=True)) + row_max
        weights = jnp.exp(scores - log_total).astype(jnp.bfloat16)
        outputs.append(
            jnp.einsum("hqk,khd->qhd", weights, value3[:stop], preferred_element_type=jnp.float32)
        )
        totals.append(log_total)
    return (jnp.concatenate(outputs, axis=0), totals)


def attend_back(query3, key3, value3, grad3, totals, block):
    length = query3.shape[0]
    scale = HEAD_DIM ** (-0.5)
    query_parts = []
    key_grad = jnp.zeros(key3.shape, jnp.float32)
    value_grad = jnp.zeros(value3.shape, jnp.float32)
    for block_id in range(length // block):
        start = block_id * block
        stop = start + block
        scores = block_scores(query3, key3, start, stop, block)
        probs = jnp.exp(scores - totals[block_id])
        g_probs = jnp.einsum(
            "qhd,khd->hqk", grad3[start:stop], value3[:stop], preferred_element_type=jnp.float32
        )
        inner = jnp.sum(probs * g_probs, axis=-1, keepdims=True)
        g_scores = (probs * (g_probs - inner)).astype(jnp.bfloat16)
        query_parts.append(
            jnp.einsum("hqk,khd->qhd", g_scores, key3[:stop], preferred_element_type=jnp.float32)
            * scale
        )
        key_grad = key_grad.at[:stop].add(
            jnp.einsum(
                "hqk,qhd->khd", g_scores, query3[start:stop], preferred_element_type=jnp.float32
            )
            * scale
        )
        value_grad = value_grad.at[:stop].add(
            jnp.einsum(
                "hqk,qhd->khd",
                probs.astype(jnp.bfloat16),
                grad3[start:stop],
                preferred_element_type=jnp.float32,
            )
        )
    return (jnp.concatenate(query_parts, axis=0), key_grad, value_grad)


def gather_attention(w_query, w_key, w_value, w_out):
    return (
        lax.all_gather(w_query, "dp", axis=0, tiled=True),
        lax.all_gather(w_key, "dp", axis=0, tiled=True),
        lax.all_gather(w_value, "dp", axis=0, tiled=True),
        lax.all_gather(w_out, "dp", axis=0, tiled=True),
    )


def gather_feedforward(w_up, w_gate, w_down):
    return (
        lax.all_gather(w_up, "dp", axis=0, tiled=True),
        lax.all_gather(w_gate, "dp", axis=0, tiled=True),
        lax.all_gather(w_down, "dp", axis=0, tiled=True),
    )


def on_device(
    tokens,
    w_query,
    w_key,
    w_value,
    w_out,
    w_up,
    w_gate,
    w_down,
    qk_scale,
    up_scale,
    gate_scale,
    alpha_attn,
    alpha_mlp,
    cotangent,
):
    query_w, key_w, value_w, out_w = gather_attention(w_query, w_key, w_value, w_out)
    whole = lax.all_gather(tokens, "tensor", axis=0, tiled=True)
    length = whole.shape[0]
    width = query_w.shape[1]
    block = min(512, length)
    cosine, sine, first_half, member = tables(width, length)
    shape3 = (length, width // HEAD_DIM, HEAD_DIM)
    q_raw = jnp.dot(whole, query_w, preferred_element_type=jnp.float32)
    k_raw = jnp.dot(whole, key_w, preferred_element_type=jnp.float32)
    value_low = jnp.dot(whole, value_w, preferred_element_type=jnp.float32).astype(jnp.bfloat16)
    q_unit, q_norm = head_unit(rope_apply(q_raw, cosine, sine, first_half), member)
    k_unit, k_norm = head_unit(rope_apply(k_raw, cosine, sine, first_half), member)
    query_low = (q_unit * qk_scale).astype(jnp.bfloat16)
    key_low = (k_unit * qk_scale).astype(jnp.bfloat16)
    query3 = query_low.reshape(shape3)
    key3 = key_low.reshape(shape3)
    value3 = value_low.reshape(shape3)
    attended, totals = attend(query3, key3, value3, block)
    attended_low = attended.reshape(length, width).astype(jnp.bfloat16)
    attn_sum = lax.psum_scatter(
        contract_cols(attended_low, out_w), "tensor", scatter_dimension=0, tiled=True
    )
    attn_unit, attn_norm = unit_rows(attn_sum)
    residual = tokens.astype(jnp.float32)
    mid, mid_norm = unit_rows(residual + alpha_attn * (attn_unit - residual))
    mid_low = mid.astype(jnp.bfloat16)
    up_w, gate_w, down_w = gather_feedforward(w_up, w_gate, w_down)
    mid_whole = lax.all_gather(mid_low, "tensor", axis=0, tiled=True)
    up_sum = jnp.dot(mid_whole, up_w, preferred_element_type=jnp.float32)
    gate_sum = jnp.dot(mid_whole, gate_w, preferred_element_type=jnp.float32)
    up_val = up_sum * up_scale
    gate_val = gate_sum * gate_scale
    sigma = jax.nn.sigmoid(gate_val)
    hidden_low = (up_val * (gate_val * sigma)).astype(jnp.bfloat16)
    mlp_sum = lax.psum_scatter(
        contract_cols(hidden_low, down_w), "tensor", scatter_dimension=0, tiled=True
    )
    mlp_unit, mlp_norm = unit_rows(mlp_sum)
    final, final_norm = unit_rows(mid + alpha_mlp * (mlp_unit - mid))
    output = final.astype(jnp.bfloat16)
    g_second = unit_back(cotangent.astype(jnp.float32), final, final_norm)
    g_alpha_mlp = jnp.sum((mlp_unit - mid) * g_second, axis=0)
    g_mlp_low = unit_back(alpha_mlp * g_second, mlp_unit, mlp_norm).astype(jnp.bfloat16)
    up_w, gate_w, down_w = gather_feedforward(w_up, w_gate, w_down)
    g_mlp_whole = lax.all_gather(g_mlp_low, "tensor", axis=0, tiled=True)
    down_grad = contract_rows(g_mlp_whole, hidden_low)
    g_hidden = jnp.dot(g_mlp_whole, down_w, preferred_element_type=jnp.float32)
    g_up = g_hidden * (gate_val * sigma)
    g_gate = g_hidden * up_val * (sigma * (1.0 + gate_val * (1.0 - sigma)))
    up_scale_grad = jnp.sum(g_up * up_sum, axis=0)
    gate_scale_grad = jnp.sum(g_gate * gate_sum, axis=0)
    g_up_low = (g_up * up_scale).astype(jnp.bfloat16)
    g_gate_low = (g_gate * gate_scale).astype(jnp.bfloat16)
    up_grad = contract_rows(mid_whole, g_up_low)
    gate_grad = contract_rows(mid_whole, g_gate_low)
    g_mid_part = contract_cols(g_up_low, up_w) + contract_cols(g_gate_low, gate_w)
    g_mid = (1.0 - alpha_mlp) * g_second + lax.psum_scatter(
        g_mid_part, "tensor", scatter_dimension=0, tiled=True
    )
    up_grad, gate_grad, down_grad = (
        lax.psum_scatter(up_grad, "dp", scatter_dimension=0, tiled=True),
        lax.psum_scatter(gate_grad, "dp", scatter_dimension=0, tiled=True),
        lax.psum_scatter(down_grad, "dp", scatter_dimension=0, tiled=True),
    )
    g_first = unit_back(g_mid, mid, mid_norm)
    g_alpha_attn = jnp.sum((attn_unit - residual) * g_first, axis=0)
    g_attn_low = unit_back(alpha_attn * g_first, attn_unit, attn_norm).astype(jnp.bfloat16)
    query_w, key_w, value_w, out_w = gather_attention(w_query, w_key, w_value, w_out)
    g_attn_whole = lax.all_gather(g_attn_low, "tensor", axis=0, tiled=True)
    out_grad = contract_rows(g_attn_whole, attended_low)
    g_attended_low = jnp.dot(g_attn_whole, out_w, preferred_element_type=jnp.float32).astype(
        jnp.bfloat16
    )
    g_query3, g_key3, g_value3 = attend_back(
        query3, key3, value3, g_attended_low.reshape(shape3), totals, block
    )
    g_query = g_query3.reshape(length, width)
    g_key = g_key3.reshape(length, width)
    qk_grad = jnp.sum(g_query * q_unit, axis=0) + jnp.sum(g_key * k_unit, axis=0)
    g_q_raw_low = rope_back(
        head_back(g_query * qk_scale, q_unit, q_norm, member), cosine, sine, first_half
    ).astype(jnp.bfloat16)
    g_k_raw_low = rope_back(
        head_back(g_key * qk_scale, k_unit, k_norm, member), cosine, sine, first_half
    ).astype(jnp.bfloat16)
    g_value_low = g_value3.reshape(length, width).astype(jnp.bfloat16)
    query_grad = contract_rows(whole, g_q_raw_low)
    key_grad = contract_rows(whole, g_k_raw_low)
    value_grad = contract_rows(whole, g_value_low)
    g_tok_part = (
        contract_cols(g_q_raw_low, query_w)
        + contract_cols(g_k_raw_low, key_w)
        + contract_cols(g_value_low, value_w)
    )
    tokens_grad = (1.0 - alpha_attn) * g_first + lax.psum_scatter(
        g_tok_part.astype(jnp.bfloat16), "tensor", scatter_dimension=0, tiled=True
    ).astype(jnp.float32)
    query_grad, key_grad, value_grad, out_grad = (
        lax.psum_scatter(query_grad, "dp", scatter_dimension=0, tiled=True),
        lax.psum_scatter(key_grad, "dp", scatter_dimension=0, tiled=True),
        lax.psum_scatter(value_grad, "dp", scatter_dimension=0, tiled=True),
        lax.psum_scatter(out_grad, "dp", scatter_dimension=0, tiled=True),
    )
    qk_grad, up_scale_grad, gate_scale_grad = lax.psum(
        (qk_grad, up_scale_grad, gate_scale_grad), "dp"
    )
    g_alpha_attn, g_alpha_mlp = lax.psum((g_alpha_attn, g_alpha_mlp), ("dp", "tensor"))
    return (
        output,
        tokens_grad,
        query_grad,
        key_grad,
        value_grad,
        out_grad,
        up_grad,
        gate_grad,
        down_grad,
        qk_grad,
        up_scale_grad,
        gate_scale_grad,
        g_alpha_attn,
        g_alpha_mlp,
    )


def solution(mesh):
    in_specs = (
        P(("dp", "tensor"), None),
        P("dp", "tensor"),
        P("dp", "tensor"),
        P("dp", "tensor"),
        P("dp", "tensor"),
        P("dp", "tensor"),
        P("dp", "tensor"),
        P("dp", "tensor"),
        P("tensor"),
        P("tensor"),
        P("tensor"),
        P(),
        P(),
        P(("dp", "tensor"), None),
    )
    out_specs = (
        P(("dp", "tensor"), None),
        P(("dp", "tensor"), None),
        P("dp", "tensor"),
        P("dp", "tensor"),
        P("dp", "tensor"),
        P("dp", "tensor"),
        P("dp", "tensor"),
        P("dp", "tensor"),
        P("dp", "tensor"),
        P("tensor"),
        P("tensor"),
        P("tensor"),
        P(),
        P(),
    )
    return jax.shard_map(
        on_device, mesh=mesh, in_specs=in_specs, out_specs=out_specs, check_vma=False
    )
```

profile of v0, /device:TPU:0, one launch (start us, length us, event | category | flops | bytes accessed | tf_op | source)
XLA Modules:
  0.0 1157.7 jit_solution(15452497443347139287)
XLA Ops:
  9.0 12.8 %all_gather.41 = bf16[1280,320]{1,0:T(8,128)(2,1)S(1)} all-gather(bf16[160,320]{1,0:T(8,128)(2,1)} %param.29), channel_id=1, replica_groups=mesh['dp'=8,'tensor'=4] {'dp'}, dimensions={0}, use_global_device_ids=true | all-gather | bytes 921600 | tf_op jit(solution)/shard_map/all_gather | solution.py:160
  21.8 11.6 %all_gather.43 = bf16[1280,320]{1,0:T(8,128)(2,1)} all-gather(bf16[160,320]{1,0:T(8,128)(2,1)S(1)} %copy-done.50), channel_id=1, replica_groups=mesh['dp'=8,'tensor'=4] {'dp'}, dimensions={0}, use_global_device_ids=true | all-gather | bytes 921600 | tf_op jit(solution)/shard_map/all_gather | solution.py:159
  33.3 11.4 all_gather.42
  44.7 11.5 all_gather.44
  56.6 11.3 all-gather.8.cloned.1.call-done
  74.3 6.9 fusion.20
  106.7 92.1 %reduce-scatter.18.cloned.1.call-done = f32[256,1280]{1,0:T(8,128)} async-done(((f32[1024,1280]{1,0:T(8,128)}), f32[256,1280]{1,0:T(8,128)}) %reduce-scatter.18.cloned.1.call-update) | async-done | bytes 1310736 | tf_op jit(solution)/shard_map/reduce_scatter | solution.py:208
  204.7 53.4 %all-gather.10.cloned.1.call-done = bf16[1024,1280]{1,0:T(8,128)(2,1)} async-done(((bf16[256,1280]{1,0:T(8,128)(2,1)}), bf16[1024,1280]{1,0:T(8,128)(2,1)}) %all-gather.10.cloned.1.call-update) | async-done | bytes 2621456 | tf_op jit(solution)/shard_map/all_gather | solution.py:216
  258.1 8.6 fusion.126
  266.7 24.5 %all-gather.12.cloned.1.call-done = bf16[1280,1280]{1,0:T(8,128)(2,1)} async-done(((bf16[160,1280]{1,0:T(8,128)(2,1)}), bf16[1280,1280]{1,0:T(8,128)(2,1)}) %all-gather.12.cloned.1.call-update) | async-done | bytes 3276816 | tf_op jit(solution)/shard_map/all_gather | solution.py:167
  291.1 11.3 multiply_convert_fusion.4
  302.5 23.2 %all-gather.16.cloned.1.call-done = bf16[1280,1280]{1,0:T(8,128)(2,1)} async-done(((bf16[160,1280]{1,0:T(8,128)(2,1)}), bf16[1280,1280]{1,0:T(8,128)(2,1)}) %all-gather.16.cloned.1.call-update) | async-done | bytes 3276816 | tf_op jit(solution)/shard_map/all_gather | solution.py:169
  325.7 8.7 fusion.127
  334.5 93.9 %reduce-scatter.20.cloned.1.call-done = f32[256,1280]{1,0:T(8,128)} async-done(((f32[1024,1280]{1,0:T(8,128)}), f32[256,1280]{1,0:T(8,128)}) %reduce-scatter.20.cloned.1.call-update) | async-done | bytes 1310736 | tf_op jit(solution)/shard_map/reduce_scatter | solution.py:223
  435.6 54.7 %all-gather.18.cloned.1.call-done = bf16[1024,1280]{1,0:T(8,128)(2,1)} async-done(((bf16[256,1280]{1,0:T(8,128)(2,1)}), bf16[1024,1280]{1,0:T(8,128)(2,1)}) %all-gather.18.cloned.1.call-update) | async-done | bytes 2621456 | tf_op jit(solution)/shard_map/all_gather | solution.py:233
  490.3 11.1 multiply_reduce_fusion.1
  505.8 5.4 convolution_add_fusion
  511.3 92.5 %reduce-scatter.22.cloned.1.call-done = f32[256,1280]{1,0:T(8,128)} async-done(((f32[1024,1280]{1,0:T(8,128)}), f32[256,1280]{1,0:T(8,128)}) %reduce-scatter.22.cloned.1.call-update) | async-done | bytes 1310736 | tf_op jit(solution)/shard_map/reduce_scatter | solution.py:245
  611.4 54.5 %all-gather.20.cloned.1.call-done = bf16[1024,1280]{1,0:T(8,128)(2,1)} async-done(((bf16[256,1280]{1,0:T(8,128)(2,1)}), bf16[1024,1280]{1,0:T(8,128)(2,1)}) %all-gather.20.cloned.1.call-update) | async-done | bytes 2621456 | tf_op jit(solution)/shard_map/all_gather | solution.py:257
  695.5 7.2 fusion.35
  705.6 5.8 fusion.24
  721.9 8.9 fusion.132
  731.1 9.7 fusion.68
  741.0 8.8 fusion.133
  779.0 39.5 %all-reduce.2 = (f32[1280]{0:T(1024)}, f32[1280]{0:T(1024)}) all-reduce(f32[1280]{0:T(1024)S(1)} %get-tuple-element.110, f32[1280]{0:T(1024)S(1)} %get-tuple-element.108), channel_id=1, replica_groups=mesh['dp'=8,'tensor'=4] {'dp','tensor'}, use_global_device_ids=true, to_apply=%region_33.34 | all-reduce | flops 2560 | bytes 20480 | tf_op jit(solution)/shard_map/psum | solution.py:295
  820.4 25.1 %all-reduce.3 = (f32[320]{0:T(512)}, f32[1280]{0:T(1024)}, f32[1280]{0:T(1024)}) all-reduce(f32[320]{0:T(512)S(1)} %add.253, f32[1280]{0:T(1024)S(1)} %get-tuple-element.107, f32[1280]{0:T(1024)S(1)} %get-tuple-element.106), channel_id=1, replica_groups=mesh['dp'=8,'tensor'=4] {'dp'}, use_global_device_ids=true, to_apply=%region_27.28 | all-reduce | flops 2880 | bytes 23040 | tf_op jit(solution)/shard_map/psum | solution.py:292
  847.8 59.0 %reduce-scatter.30.cloned.1.call-done = f32[160,1280]{1,0:T(8,128)} async-done(((f32[1280,1280]{1,0:T(8,128)}), f32[160,1280]{1,0:T(8,128)}) %reduce-scatter.30.cloned.1.call-update) | async-done | bytes 819216 | tf_op jit(solution)/shard_map/reduce_scatter | solution.py:250
  906.9 66.9 %reduce-scatter.32.cloned.1.call-done = f32[160,1280]{1,0:T(8,128)} async-done(((f32[1280,1280]{1,0:T(8,128)}), f32[160,1280]{1,0:T(8,128)}) %reduce-scatter.32.cloned.1.call-update) | async-done | bytes 819216 | tf_op jit(solution)/shard_map/reduce_scatter | solution.py:251
  973.8 43.9 %reduce-scatter.34.cloned.1.call-done = f32[160,320]{1,0:T(8,128)} async-done(((f32[1280,320]{1,0:T(8,128)}), f32[160,320]{1,0:T(8,128)}) %reduce-scatter.34.cloned.1.call-update) | async-done | bytes 204816
  1017.7 44.1 %reduce-scatter.36.cloned.1.call-done = f32[160,320]{1,0:T(8,128)} async-done(((f32[1280,320]{1,0:T(8,128)}), f32[160,320]{1,0:T(8,128)}) %reduce-scatter.36.cloned.1.call-update) | async-done | bytes 204816
  1061.8 43.9 %reduce-scatter.38.cloned.1.call-done = f32[160,320]{1,0:T(8,128)} async-done(((f32[1280,320]{1,0:T(8,128)}), f32[160,320]{1,0:T(8,128)}) %reduce-scatter.38.cloned.1.call-update) | async-done | bytes 204816
  1105.7 44.1 %reduce-scatter.26.cloned.1.call-done = f32[160,320]{1,0:T(8,128)} async-done(((f32[1280,320]{1,0:T(8,128)}), f32[160,320]{1,0:T(8,128)}) %reduce-scatter.26.cloned.1.call-update) | async-done | bytes 204816 | tf_op jit(solution)/shard_map/reduce_scatter | solution.py:290
  (260 shorter events, 134.3 us)
Async XLA Ops:
  8.0 13.7 %copy-start.50 = (bf16[160,320]{1,0:T(8,128)(2,1)S(1)}, bf16[160,320]{1,0:T(8,128)(2,1)}, u32[]{:S(2)}) copy-start(bf16[160,320]{1,0:T(8,128)(2,1)} %param.28) | copy-start | bytes 307204
  8.0 25.3 %copy-start.51 = (bf16[160,320]{1,0:T(8,128)(2,1)S(1)}, bf16[160,320]{1,0:T(8,128)(2,1)}, u32[]{:S(2)}) copy-start(bf16[160,320]{1,0:T(8,128)(2,1)} %param.27) | copy-start | bytes 307204
  8.0 59.9 %all-gather.8.cloned.1.call-start = ((), (), s32[]{:S(2)}) async-start(), calls=%async_computation.11 | async-start | bytes 3276800 | tf_op jit(solution)/shard_map/all_gather | solution.py:190
  8.8 190.0 %reduce-scatter.18.cloned.1.call-start = ((), (), s32[]{:S(2)}) async-start(), calls=%async_computation.12 | async-start | bytes 6553600 | tf_op jit(solution)/shard_map/reduce_scatter | solution.py:208
  9.0 35.8 %copy-start.52 = (bf16[160,320]{1,0:T(8,128)(2,1)S(1)}, bf16[160,320]{1,0:T(8,128)(2,1)}, u32[]{:S(2)}) copy-start(bf16[160,320]{1,0:T(8,128)(2,1)} %param.30) | copy-start | bytes 307204
  21.8 71.2 %copy-start.24 = (bf16[1280,320]{1,0:T(8,128)(2,1)}, bf16[1280,320]{1,0:T(8,128)(2,1)S(1)}, u32[]{:S(2)}) copy-start(bf16[1280,320]{1,0:T(8,128)(2,1)S(1)} %all_gather.41) | copy-start | bytes 2457604
  106.1 94.3 %copy-start.49 = (f32[1280]{0:T(1024)S(1)}, f32[1280]{0:T(1024)}, u32[]{:S(2)}) copy-start(f32[1280]{0:T(1024)} %param.37) | copy-start | bytes 15364
  106.1 98.6 %all-gather.14.cloned.1.call-start = ((), (), s32[]{:S(2)}) async-start(), calls=%async_computation.15 | async-start | bytes 3686400 | tf_op jit(solution)/shard_map/all_gather | solution.py:168
  106.7 151.4 %all-gather.10.cloned.1.call-start = ((), (), s32[]{:S(2)}) async-start(), calls=%async_computation.13 | async-start | bytes 3276800 | tf_op jit(solution)/shard_map/all_gather | solution.py:216
  203.1 88.0 %all-gather.12.cloned.1.call-start = ((), (), s32[]{:S(2)}) async-start(), calls=%async_computation.14 | async-start | bytes 3686400 | tf_op jit(solution)/shard_map/all_gather | solution.py:167
  203.7 122.0 %all-gather.16.cloned.1.call-start = ((), (), s32[]{:S(2)}) async-start(), calls=%async_computation.16 | async-start | bytes 3686400 | tf_op jit(solution)/shard_map/all_gather | solution.py:169
  204.4 86.7 %copy-start.57 = (f32[1280]{0:T(1024)S(1)}, f32[1280]{0:T(1024)}, u32[]{:S(2)}) copy-start(f32[1280]{0:T(1024)} %param.35) | copy-start | bytes 15364
  204.4 86.7 %copy-start.58 = (f32[1280]{0:T(1024)S(1)}, f32[1280]{0:T(1024)}, u32[]{:S(2)}) copy-start(f32[1280]{0:T(1024)} %param.36) | copy-start | bytes 15364
  204.4 223.9 %reduce-scatter.20.cloned.1.call-start = ((), (), s32[]{:S(2)}) async-start(), calls=%async_computation.17 | async-start | bytes 6553600 | tf_op jit(solution)/shard_map/reduce_scatter | solution.py:223
  334.4 95.6 %copy-start.48 = (f32[1280]{0:T(1024)S(1)}, f32[1280]{0:T(1024)}, u32[]{:S(2)}) copy-start(f32[1280]{0:T(1024)} %param.38) | copy-start | bytes 15364
  334.4 155.9 %all-gather.18.cloned.1.call-start = ((), (), s32[]{:S(2)}) async-start(), calls=%async_computation.18 | async-start | bytes 3276800 | tf_op jit(solution)/shard_map/all_gather | solution.py:233
  435.3 168.5 %reduce-scatter.22.cloned.1.call-start = ((), (), s32[]{:S(2)}) async-start(), calls=%async_computation.19 | async-start | bytes 6553600 | tf_op jit(solution)/shard_map/reduce_scatter | solution.py:245
  490.3 11.1 copy-start.55
  511.2 154.7 %all-gather.20.cloned.1.call-start = ((), (), s32[]{:S(2)}) async-start(), calls=%async_computation.20 | async-start | bytes 3276800 | tf_op jit(solution)/shard_map/all_gather | solution.py:257
  609.7 56.2 %copy-start.30 = (bf16[1280,320]{1,0:T(8,128)(2,1)S(1)}, bf16[1280,320]{1,0:T(8,128)(2,1)}, u32[]{:S(2)}) copy-start(bf16[1280,320]{1,0:T(8,128)(2,1)} %all_gather.44) | copy-start | bytes 2457604
  610.8 58.6 %copy-start.43 = (bf16[512,320]{0,1:T(8,128)(2,1)S(1)}, bf16[512,320]{0,1:T(8,128)(2,1)}, u32[]{:S(2)}) copy-start(bf16[512,320]{0,1:T(8,128)(2,1)} %copy-done.42) | copy-start | bytes 983044
  610.9 234.7 %reduce-scatter.24.cloned.1.call-start = ((), (), s32[]{:S(2)}) async-start(), calls=%async_computation.21 | async-start | bytes 3276800 | tf_op jit(solution)/shard_map/reduce_scatter | solution.py:283
  669.5 10.7 slice-start
  669.5 10.7 slice-start.1
  721.9 125.9 %reduce-scatter.28.cloned.1.call-start = ((), (), s32[]{:S(2)}) async-start(), calls=%async_computation.23 | async-start | bytes 7372800 | tf_op jit(solution)/shard_map/reduce_scatter | solution.py:249
  730.8 176.0 %reduce-scatter.30.cloned.1.call-start = ((), (), s32[]{:S(2)}) async-start(), calls=%async_computation.24 | async-start | bytes 7372800 | tf_op jit(solution)/shard_map/reduce_scatter | solution.py:250
  740.9 232.9 %reduce-scatter.32.cloned.1.call-start = ((), (), s32[]{:S(2)}) async-start(), calls=%async_computation.25 | async-start | bytes 7372800 | tf_op jit(solution)/shard_map/reduce_scatter | solution.py:251
  749.8 267.9 %reduce-scatter.34.cloned.1.call-start = ((), (), s32[]{:S(2)}) async-start(), calls=%async_computation.26 | async-start | bytes 2211840
  757.7 304.1 %reduce-scatter.36.cloned.1.call-start = ((), (), s32[]{:S(2)}) async-start(), calls=%async_computation.27 | async-start | bytes 2211840
  765.5 340.2 %reduce-scatter.38.cloned.1.call-start = ((), (), s32[]{:S(2)}) async-start(), calls=%async_computation.28 | async-start | bytes 2211840
  773.3 376.5 %reduce-scatter.26.cloned.1.call-start = ((), (), s32[]{:S(2)}) async-start(), calls=%async_computation.22 | async-start | bytes 2211840 | tf_op jit(solution)/shard_map/reduce_scatter | solution.py:290
  820.2 25.4 %copy-start.13 = (f32[256,1280]{1,0:T(8,128)S(1)}, f32[256,1280]{1,0:T(8,128)}, u32[]{:S(2)}) copy-start(f32[256,1280]{1,0:T(8,128)} %copy-done.12) | copy-start | bytes 3932164
  (52 other events, 136.5 us)
Sparse Core Ops, SparseCore 0:
  10.4 57.4 all-gather.7
  106.2 92.5 reduce-scatter.17
  334.5 93.7 reduce-scatter.19
  511.3 92.3 reduce-scatter.21
Sparse Core Ops, SparseCore 1:
  108.5 31.4 all-gather.13
  203.2 54.9 all-gather.9
  259.9 31.2 all-gather.11
  293.0 32.6 all-gather.15
  435.3 54.9 all-gather.17
  610.9 54.9 all-gather.19
  722.0 50.8 reduce-scatter.23
  776.7 63.3 reduce-scatter.27
  843.9 62.9 reduce-scatter.29
  910.9 62.8 reduce-scatter.31
  977.6 40.0 reduce-scatter.33
  1021.7 40.0 reduce-scatter.35
  1065.6 40.0 reduce-scatter.37
  1109.7 40.0 reduce-scatter.25
where the time goes:
time: 1160 us
  waiting for transfers between devices  805 us (69%)
  matrix products  153 us (13%)
  blocking collectives  112 us (10%)
  other arithmetic  43.9 us (4%)
  local copies, waits for them, and re-layouts  24.3 us (2%)
  between operations  17.2 us (1%)
    unnamed x21, waiting for transfers between devices  135 us
    reduce_scatter x1, waiting for transfers between devices, on_device(): lax.psum_scatter(contract_cols(hidden_low, down_w), 'tensor', scatter_dim...  93.9 us
    reduce_scatter x1, waiting for transfers between devices, on_device(): lax.psum_scatter(g_mid_part, 'tensor', scatter_dimension=0, tiled=True)  92.5 us
    reduce_scatter x1, waiting for transfers between devices, on_device(): lax.psum_scatter(contract_cols(attended_low, out_w), 'tensor', scatter_di...  92.1 us
    reduce_scatter x1, waiting for transfers between devices, on_device(): lax.psum_scatter(down_grad, 'dp', scatter_dimension=0, tiled=True)  66.9 us
    reduce_scatter x1, waiting for transfers between devices, on_device(): lax.psum_scatter(gate_grad, 'dp', scatter_dimension=0, tiled=True)  59 us
    all_gather x1, waiting for transfers between devices, on_device(): g_mlp_whole = lax.all_gather(g_mlp_low, 'tensor', axis=0, tiled=True)  54.7 us
    all_gather x1, waiting for transfers between devices, on_device(): g_attn_whole = lax.all_gather(g_attn_low, 'tensor', axis=0, tiled=True)  54.5 us
  transfers between devices with their start and end apart: 18, of which 15 were waited for; matrix products, arithmetic and copies ran while one was open for 7% of the time, Pallas kernels for 0%

commit v1 on v0

--- a/solution.py
+++ b/solution.py
@@ -153,21 +153,10 @@
     return (jnp.concatenate(query_parts, axis=0), key_grad, value_grad)
 
 
-def gather_attention(w_query, w_key, w_value, w_out):
-    return (
-        lax.all_gather(w_query, "dp", axis=0, tiled=True),
-        lax.all_gather(w_key, "dp", axis=0, tiled=True),
-        lax.all_gather(w_value, "dp", axis=0, tiled=True),
-        lax.all_gather(w_out, "dp", axis=0, tiled=True),
-    )
-
-
-def gather_feedforward(w_up, w_gate, w_down):
-    return (
-        lax.all_gather(w_up, "dp", axis=0, tiled=True),
-        lax.all_gather(w_gate, "dp", axis=0, tiled=True),
-        lax.all_gather(w_down, "dp", axis=0, tiled=True),
-    )
+def scatter_low(value, axis):
+    return lax.psum_scatter(
+        value.astype(jnp.bfloat16), axis, scatter_dimension=0, tiled=True
+    ).astype(jnp.float32)
 
 
 def on_device(
@@ -186,8 +175,15 @@
     alpha_mlp,
     cotangent,
 ):
-    query_w, key_w, value_w, out_w = gather_attention(w_query, w_key, w_value, w_out)
+    attn_w = lax.all_gather(
+        jnp.concatenate([w_query, w_key, w_value, w_out], axis=1), "dp", axis=0, tiled=True
+    )
+    query_w, key_w, value_w, out_w = jnp.split(attn_w, 4, axis=1)
     whole = lax.all_gather(tokens, "tensor", axis=0, tiled=True)
+    mlp_w = lax.all_gather(
+        jnp.concatenate([w_up, w_gate, w_down], axis=1), "dp", axis=0, tiled=True
+    )
+    up_w, gate_w, down_w = jnp.split(mlp_w, 3, axis=1)
     length = whole.shape[0]
     width = query_w.shape[1]
     block = min(512, length)
@@ -205,14 +201,11 @@
     value3 = value_low.reshape(shape3)
     attended, totals = attend(query3, key3, value3, block)
     attended_low = attended.reshape(length, width).astype(jnp.bfloat16)
-    attn_sum = lax.psum_scatter(
-        contract_cols(attended_low, out_w), "tensor", scatter_dimension=0, tiled=True
-    )
+    attn_sum = scatter_low(contract_cols(attended_low, out_w), "tensor")
     attn_unit, attn_norm = unit_rows(attn_sum)
     residual = tokens.astype(jnp.float32)
     mid, mid_norm = unit_rows(residual + alpha_attn * (attn_unit - residual))
     mid_low = mid.astype(jnp.bfloat16)
-    up_w, gate_w, down_w = gather_feedforward(w_up, w_gate, w_down)
     mid_whole = lax.all_gather(mid_low, "tensor", axis=0, tiled=True)
     up_sum = jnp.dot(mid_whole, up_w, preferred_element_type=jnp.float32)
     gate_sum = jnp.dot(mid_whole, gate_w, preferred_element_type=jnp.float32)
@@ -220,16 +213,13 @@
     gate_val = gate_sum * gate_scale
     sigma = jax.nn.sigmoid(gate_val)
     hidden_low = (up_val * (gate_val * sigma)).astype(jnp.bfloat16)
-    mlp_sum = lax.psum_scatter(
-        contract_cols(hidden_low, down_w), "tensor", scatter_dimension=0, tiled=True
-    )
+    mlp_sum = scatter_low(contract_cols(hidden_low, down_w), "tensor")
     mlp_unit, mlp_norm = unit_rows(mlp_sum)
     final, final_norm = unit_rows(mid + alpha_mlp * (mlp_unit - mid))
     output = final.astype(jnp.bfloat16)
     g_second = unit_back(cotangent.astype(jnp.float32), final, final_norm)
     g_alpha_mlp = jnp.sum((mlp_unit - mid) * g_second, axis=0)
     g_mlp_low = unit_back(alpha_mlp * g_second, mlp_unit, mlp_norm).astype(jnp.bfloat16)
-    up_w, gate_w, down_w = gather_feedforward(w_up, w_gate, w_down)
     g_mlp_whole = lax.all_gather(g_mlp_low, "tensor", axis=0, tiled=True)
     down_grad = contract_rows(g_mlp_whole, hidden_low)
     g_hidden = jnp.dot(g_mlp_whole, down_w, preferred_element_type=jnp.float32)
@@ -242,18 +232,13 @@
     up_grad = contract_rows(mid_whole, g_up_low)
     gate_grad = contract_rows(mid_whole, g_gate_low)
     g_mid_part = contract_cols(g_up_low, up_w) + contract_cols(g_gate_low, gate_w)
-    g_mid = (1.0 - alpha_mlp) * g_second + lax.psum_scatter(
-        g_mid_part, "tensor", scatter_dimension=0, tiled=True
-    )
-    up_grad, gate_grad, down_grad = (
-        lax.psum_scatter(up_grad, "dp", scatter_dimension=0, tiled=True),
-        lax.psum_scatter(gate_grad, "dp", scatter_dimension=0, tiled=True),
-        lax.psum_scatter(down_grad, "dp", scatter_dimension=0, tiled=True),
+    g_mid = (1.0 - alpha_mlp) * g_second + scatter_low(g_mid_part, "tensor")
+    up_grad, gate_grad, down_grad = jnp.split(
+        scatter_low(jnp.concatenate([up_grad, gate_grad, down_grad], axis=1), "dp"), 3, axis=1
     )
     g_first = unit_back(g_mid, mid, mid_norm)
     g_alpha_attn = jnp.sum((attn_unit - residual) * g_first, axis=0)
     g_attn_low = unit_back(alpha_attn * g_first, attn_unit, attn_norm).astype(jnp.bfloat16)
-    query_w, key_w, value_w, out_w = gather_attention(w_query, w_key, w_value, w_out)
     g_attn_whole = lax.all_gather(g_attn_low, "tensor", axis=0, tiled=True)
     out_grad = contract_rows(g_attn_whole, attended_low)
     g_attended_low = jnp.dot(g_attn_whole, out_w, preferred_element_type=jnp.float32).astype(
@@ -283,16 +268,27 @@
     tokens_grad = (1.0 - alpha_attn) * g_first + lax.psum_scatter(
         g_tok_part.astype(jnp.bfloat16), "tensor", scatter_dimension=0, tiled=True
     ).astype(jnp.float32)
-    query_grad, key_grad, value_grad, out_grad = (
-        lax.psum_scatter(query_grad, "dp", scatter_dimension=0, tiled=True),
-        lax.psum_scatter(key_grad, "dp", scatter_dimension=0, tiled=True),
-        lax.psum_scatter(value_grad, "dp", scatter_dimension=0, tiled=True),
-        lax.psum_scatter(out_grad, "dp", scatter_dimension=0, tiled=True),
-    )
-    qk_grad, up_scale_grad, gate_scale_grad = lax.psum(
-        (qk_grad, up_scale_grad, gate_scale_grad), "dp"
-    )
-    g_alpha_attn, g_alpha_mlp = lax.psum((g_alpha_attn, g_alpha_mlp), ("dp", "tensor"))
+    query_grad, key_grad, value_grad, out_grad = jnp.split(
+        scatter_low(
+            jnp.concatenate([query_grad, key_grad, value_grad, out_grad], axis=1), "dp"
+        ),
+        4,
+        axis=1,
+    )
+    sizes = (g_alpha_attn.shape[0], g_alpha_mlp.shape[0], up_scale_grad.shape[0], gate_scale_grad.shape[0])
+    cuts = (sizes[0], sizes[0] + sizes[1], sum(sizes[:3]), sum(sizes))
+    small = jnp.sum(
+        lax.all_gather(
+            jnp.concatenate([g_alpha_attn, g_alpha_mlp, up_scale_grad, gate_scale_grad, qk_grad]),
+            "dp",
+        ),
+        axis=0,
+    )
+    alphas = jnp.sum(lax.all_gather(small[: cuts[1]], "tensor"), axis=0)
+    g_alpha_attn, g_alpha_mlp = alphas[: cuts[0]], alphas[cuts[0] :]
+    up_scale_grad = small[cuts[1] : cuts[2]]
+    gate_scale_grad = small[cuts[2] : cuts[3]]
+    qk_grad = small[cuts[3] :]
     return (
         output,
         tokens_grad,

time: 1160 us -> 893 us (0.77)
  waiting for transfers between devices: 805 us -> 622 us
  blocking collectives: 112 us -> 13.1 us
  local copies, waits for them, and re-layouts: 24.3 us -> 54 us
  matrix products: 153 us -> 124 us
  other arithmetic: 43.9 us -> 57.6 us
    reduce_scatter x7 -> x3, waiting for transfers between devices: 448 us -> 155 us  [scatter_low(): lax.psum_scatter(value.astype(jnp.bfloat16), axis, scatter_dimension=0, t...]
    psum x2 -> x0, blocking collectives: 64.6 us -> none  [the longest x1 39.5 us: on_device(): lax.psum((g_alpha_attn, g_alpha_mlp), ('dp', 'tensor'))]
    reduce_scatter x1, waiting for transfers between devices: 0.01 us -> 49.8 us  [on_device(): lax.psum_scatter(g_tok_part.astype(jnp.bfloat16), 'tensor', scatter_dimen...]
    all_gather x3 -> x2, waiting for transfers between devices: 47.7 us -> 94.9 us  [the longest x1 60.9 us: on_device(): lax.all_gather(jnp.concatenate([w_up, w_gate, w_down], axis=1), 'dp', axi...]
    all_gather x1, waiting for transfers between devices: 11.3 us -> 55.9 us  [on_device(): whole = lax.all_gather(tokens, 'tensor', axis=0, tiled=True)]
    all_gather x4 -> x1, blocking collectives: 47.2 us -> 13.1 us  [on_device(): alphas = jnp.sum(lax.all_gather(small[:cuts[1]], 'tensor'), axis=0)]
    unnamed x21 -> x16, waiting for transfers between devices: 135 us -> 108 us
    dot_general x7, matrix products: 43.8 us -> 18.2 us  [contract_rows(): lax.dot_general(left, right, (((0,), (0,)), ((), ())), preferred_element_...]
  transfers between devices with their start and end apart: 18 -> 13, of which waited for: 15 -> 12; matrix products, arithmetic and copies ran while one was open for 7% -> 8% of each run, Pallas kernels for 0% -> 0%
where the time goes in v1:
time: 893 us; the launch traced here: 888 us
  waiting for transfers between devices  622 us (70%)
  matrix products  124 us (14%)
  other arithmetic  57.6 us (6%)
  local copies, waits for them, and re-layouts  54 us (6%)
  between operations  16.4 us (2%)
  blocking collectives  13.1 us (1%)
    reduce_scatter x3, waiting for transfers between devices, scatter_low(): lax.psum_scatter(value.astype(jnp.bfloat16), axis, scatter_dimension=0, t...  155 us
    unnamed x16, waiting for transfers between devices  108 us
    all_gather x1, waiting for transfers between devices, on_device(): lax.all_gather(jnp.concatenate([w_up, w_gate, w_down], axis=1), 'dp', axi...  60.9 us
    all_gather x1, waiting for transfers between devices, on_device(): whole = lax.all_gather(tokens, 'tensor', axis=0, tiled=True)  55.9 us
    all_gather x1, waiting for transfers between devices, on_device(): g_mlp_whole = lax.all_gather(g_mlp_low, 'tensor', axis=0, tiled=True)  54.4 us
    all_gather x1, waiting for transfers between devices, on_device(): g_attn_whole = lax.all_gather(g_attn_low, 'tensor', axis=0, tiled=True)  53 us
    all_gather x1, waiting for transfers between devices, on_device(): mid_whole = lax.all_gather(mid_low, 'tensor', axis=0, tiled=True)  52.1 us
    reduce_scatter x1, waiting for transfers between devices, on_device(): lax.psum_scatter(g_tok_part.astype(jnp.bfloat16), 'tensor', scatter_dimen...  49.8 us
  transfers between devices with their start and end apart: 13, of which 12 were waited for; matrix products, arithmetic and copies ran while one was open for 8% of the time, Pallas kernels for 0%

profile of v1, /device:TPU:0, one launch (start us, length us, event | category | flops | bytes accessed | tf_op | source)
XLA Modules:
  0.0 888.2 jit_solution(8824754908947580795)
XLA Ops:
  11.2 55.9 %all-gather.12.cloned.1.call-done = bf16[1024,1280]{1,0:T(8,128)(2,1)} async-done(((bf16[256,1280]{1,0:T(8,128)(2,1)}), bf16[1024,1280]{1,0:T(8,128)(2,1)}) %all-gather.12.cloned.1.call-update) | async-done | bytes 2621456 | tf_op jit(solution)/shard_map/all_gather | solution.py:182
  67.1 34.0 %all-gather.10.cloned.1.call-done = bf16[1280,1280]{1,0:T(8,128)(2,1)} async-done(((bf16[160,1280]{1,0:T(8,128)(2,1)}), bf16[1280,1280]{1,0:T(8,128)(2,1)}) %all-gather.10.cloned.1.call-update) | async-done | bytes 3276816 | tf_op jit(solution)/shard_map/all_gather | solution.py:178
  101.0 3.9 convolution_bitcast_fusion.1
  107.1 6.5 fusion.49
  138.4 52.4 %reduce-scatter.11.cloned.1.call-done = bf16[256,1280]{1,0:T(8,128)(2,1)} async-done(((bf16[1024,1280]{1,0:T(8,128)(2,1)}), bf16[256,1280]{1,0:T(8,128)(2,1)}) %reduce-scatter.11.cloned.1.call-update) | async-done | bytes 655376 | tf_op jit(solution)/shard_map/reduce_scatter | solution.py:157
  197.6 52.1 %all-gather.14.cloned.1.call-done = bf16[1024,1280]{1,0:T(8,128)(2,1)} async-done(((bf16[256,1280]{1,0:T(8,128)(2,1)}), bf16[1024,1280]{1,0:T(8,128)(2,1)}) %all-gather.14.cloned.1.call-update) | async-done | bytes 2621456 | tf_op jit(solution)/shard_map/all_gather | solution.py:209
  249.6 60.9 %all-gather.16.cloned.1.call-done = bf16[1280,3840]{1,0:T(8,128)(2,1)} async-done(((bf16[160,3840]{1,0:T(8,128)(2,1)}), bf16[1280,3840]{1,0:T(8,128)(2,1)}) %all-gather.16.cloned.1.call-update) | async-done | bytes 9830416 | tf_op jit(solution)/shard_map/all_gather | solution.py:183
  310.5 6.4 fusion.8
  317.0 5.7 multiply_convert_fusion.4
  324.2 4.9 convolution_convert_fusion.3
  329.6 52.0 %reduce-scatter.13.cloned.1.call-done = bf16[256,1280]{1,0:T(8,128)(2,1)} async-done(((bf16[1024,1280]{1,0:T(8,128)(2,1)}), bf16[256,1280]{1,0:T(8,128)(2,1)}) %reduce-scatter.13.cloned.1.call-update) | async-done | bytes 655376 | tf_op jit(solution)/shard_map/reduce_scatter | solution.py:157
  390.1 54.4 %all-gather.18.cloned.1.call-done = bf16[1024,1280]{1,0:T(8,128)(2,1)} async-done(((bf16[256,1280]{1,0:T(8,128)(2,1)}), bf16[1024,1280]{1,0:T(8,128)(2,1)}) %all-gather.18.cloned.1.call-update) | async-done | bytes 2621456 | tf_op jit(solution)/shard_map/all_gather | solution.py:223
  444.5 10.8 %multiply_reduce_fusion.1 = (f32[1280]{0:T(1024)}, f32[1280]{0:T(1024)}, f32[1024,1280]{1,0:T(8,128)S(1)}, bf16[1024,1280]{1,0:T(8,128)(2,1)S(1)}) fusion(f32[1024,1280]{1,0:T(8,128)} %copy-done.96, f32[1024,1280]{1,0:T(8,128)} %get-tuple-element.179, f32[1280]{0:T(1024)} %param.36, f32[1280]{0:T(1024)} %param.35, ...), kind=kOutput, calls=%fused_computation.11 | convolution fusion | flops 3380344320 | bytes 24274944 | tf_op jit(solution)/shard_map/dot_general | solution.py:225
  455.3 8.0 fusion.10
  463.4 7.0 add_convert_fusion.1
  471.2 50.4 %reduce-scatter.15.cloned.1.call-done = bf16[256,1280]{1,0:T(8,128)(2,1)} async-done(((bf16[1024,1280]{1,0:T(8,128)(2,1)}), bf16[256,1280]{1,0:T(8,128)(2,1)}) %reduce-scatter.15.cloned.1.call-update) | async-done | bytes 655376 | tf_op jit(solution)/shard_map/reduce_scatter | solution.py:157
  531.7 53.0 %all-gather.20.cloned.1.call-done = bf16[1024,1280]{1,0:T(8,128)(2,1)} async-done(((bf16[256,1280]{1,0:T(8,128)(2,1)}), bf16[1024,1280]{1,0:T(8,128)(2,1)}) %all-gather.20.cloned.1.call-update) | async-done | bytes 2621456 | tf_op jit(solution)/shard_map/all_gather | solution.py:242
  589.2 4.5 multiply_reduce_fusion.3
  593.7 4.2 multiply_convert_fusion.1
  600.2 3.8 multiply_reduce_fusion
  615.3 6.4 fusion.64
  628.5 3.8 fusion.31
  633.6 7.5 fusion.53
  659.8 6.3 convolution_convert_fusion
  666.1 3.9 convolution_convert_fusion.2
  670.1 4.0 convolution_convert_fusion.1
  674.1 4.7 pad_maximum_fusion
  678.8 13.7 %copy.67 = bf16[1280,3840]{1,0:T(8,128)(2,1)} copy(bf16[1280,3840]{0,1:T(8,128)(2,1)} %pad_maximum_fusion) | data formatting | bytes 19660800
  694.2 13.1 %all-gather.2 = f32[4,1,2560]{2,1,0:T(1,128)S(1)} all-gather(f32[1,1,2560]{2,1,0:T(1,128)S(1)} %reshape.307), channel_id=3, replica_groups=mesh['dp'=8,'tensor'=4] {'tensor'}, dimensions={0}, use_global_device_ids=true | all-gather | bytes 51200 | tf_op jit(solution)/shard_map/all_gather | solution.py:287
  708.6 27.1 %reduce-scatter.19.cloned.1.call-done = bf16[160,1280]{1,0:T(8,128)(2,1)} async-done(((bf16[1280,1280]{1,0:T(8,128)(2,1)}), bf16[160,1280]{1,0:T(8,128)(2,1)}) %reduce-scatter.19.cloned.1.call-update) | async-done | bytes 409616
  740.4 49.8 %reduce-scatter.17.cloned.1.call-done = bf16[256,1280]{1,0:T(8,128)(2,1)} async-done(((bf16[1024,1280]{1,0:T(8,128)(2,1)}), bf16[256,1280]{1,0:T(8,128)(2,1)}) %reduce-scatter.17.cloned.1.call-update) | async-done | bytes 655376 | tf_op jit(solution)/shard_map/reduce_scatter | solution.py:268
  792.5 79.5 %reduce-scatter.21.cloned.1.call-done = bf16[160,3840]{1,0:T(8,128)(2,1)} async-done(((bf16[1280,3840]{1,0:T(8,128)(2,1)}), bf16[160,3840]{1,0:T(8,128)(2,1)}) %reduce-scatter.21.cloned.1.call-update) | async-done | bytes 1228816
  (351 shorter events, 121.3 us)
Async XLA Ops:
  7.2 59.9 %all-gather.12.cloned.1.call-start = ((), (), s32[]{:S(2)}) async-start(), calls=%async_computation.7 | async-start | bytes 3276800 | tf_op jit(solution)/shard_map/all_gather | solution.py:182
  7.9 93.1 %all-gather.10.cloned.1.call-start = ((), (), s32[]{:S(2)}) async-start(), calls=%async_computation.6 | async-start | bytes 3686400 | tf_op jit(solution)/shard_map/all_gather | solution.py:178
  10.0 180.8 %reduce-scatter.11.cloned.1.call-start = ((), (), s32[]{:S(2)}) async-start(), calls=%async_computation.8 | async-start | bytes 3276800 | tf_op jit(solution)/shard_map/reduce_scatter | solution.py:157
  10.6 105.2 %copy-start.70 = (pred[320]{0:T(512)(128)(4,1)}, pred[320]{0:T(512)(128)(4,1)S(1)}, u32[]{:S(2)}) copy-start(pred[320]{0:T(512)(128)(4,1)S(1)} %fusion.146) | copy-start | bytes 964
  10.7 96.4 %copy-start.74 = (f32[320]{0:T(512)}, f32[320]{0:T(512)S(1)}, u32[]{:S(2)}) copy-start(f32[320]{0:T(512)S(1)} %fusion.140) | copy-start | bytes 3844
  10.7 105.1 %copy-start.49 = (s32[320]{0:T(512)}, s32[320]{0:T(512)S(1)}, u32[]{:S(2)}) copy-start(s32[320]{0:T(512)S(1)} %get-tuple-element.189) | copy-start | bytes 3844
  10.7 105.1 %copy-start.51 = (s32[320]{0:T(512)}, s32[320]{0:T(512)S(1)}, u32[]{:S(2)}) copy-start(s32[320]{0:T(512)S(1)} %get-tuple-element.190) | copy-start | bytes 3844
  11.2 118.2 %copy-start.8 = (pred[512,1024]{1,0:T(8,128)(4,1)}, pred[512,1024]{1,0:T(8,128)(4,1)S(1)}, u32[]{:S(2)}) copy-start(pred[512,1024]{1,0:T(8,128)(4,1)S(1)} %iota_compare_fusion) | copy-start | bytes 1572868
  67.1 37.9 %copy-start.85 = (bf16[1024,1280]{1,0:T(8,128)(2,1)S(1)}, bf16[1024,1280]{1,0:T(8,128)(2,1)}, u32[]{:S(2)}) copy-start(bf16[1024,1280]{1,0:T(8,128)(2,1)} %all-gather.12.cloned.1.call-done) | copy-start | bytes 7864324
  118.4 8.8 copy-start.27
  120.5 9.0 %copy-start = (f32[5,512,1024]{2,1,0:T(8,128)}, f32[5,512,1024]{2,1,0:T(8,128)S(1)}, u32[]{:S(2)}) copy-start(f32[5,512,1024]{2,1,0:T(8,128)S(1)} %get-tuple-element.175) | copy-start | bytes 31457284
  138.4 53.8 %copy-start.3 = (bf16[256,1280]{1,0:T(8,128)(2,1)S(1)}, bf16[256,1280]{1,0:T(8,128)(2,1)}, u32[]{:S(2)}) copy-start(bf16[256,1280]{1,0:T(8,128)(2,1)} %param.26) | copy-start | bytes 1966084
  138.4 53.8 %copy-start.41 = (f32[1280]{0:T(1024)S(1)}, f32[1280]{0:T(1024)}, u32[]{:S(2)}) copy-start(f32[1280]{0:T(1024)} %param.37) | copy-start | bytes 15364
  138.4 111.3 %all-gather.14.cloned.1.call-start = ((), (), s32[]{:S(2)}) async-start(), calls=%async_computation.9 | async-start | bytes 3276800 | tf_op jit(solution)/shard_map/all_gather | solution.py:209
  195.2 115.3 %all-gather.16.cloned.1.call-start = ((), (), s32[]{:S(2)}) async-start(), calls=%async_computation.10 | async-start | bytes 11059200 | tf_op jit(solution)/shard_map/all_gather | solution.py:183
  197.5 119.5 %copy-start.90 = (f32[1280]{0:T(1024)S(1)}, f32[1280]{0:T(1024)}, u32[]{:S(2)}) copy-start(f32[1280]{0:T(1024)} %param.35) | copy-start | bytes 15364
  197.5 119.5 %copy-start.91 = (f32[1280]{0:T(1024)S(1)}, f32[1280]{0:T(1024)}, u32[]{:S(2)}) copy-start(f32[1280]{0:T(1024)} %param.36) | copy-start | bytes 15364
  197.5 184.0 %reduce-scatter.13.cloned.1.call-start = ((), (), s32[]{:S(2)}) async-start(), calls=%async_computation.11 | async-start | bytes 3276800 | tf_op jit(solution)/shard_map/reduce_scatter | solution.py:157
  329.1 53.8 %copy-start.48 = (f32[1280]{0:T(1024)S(1)}, f32[1280]{0:T(1024)}, u32[]{:S(2)}) copy-start(f32[1280]{0:T(1024)} %param.38) | copy-start | bytes 15364
  329.1 115.4 %all-gather.18.cloned.1.call-start = ((), (), s32[]{:S(2)}) async-start(), calls=%async_computation.12 | async-start | bytes 3276800 | tf_op jit(solution)/shard_map/all_gather | solution.py:223
  390.0 131.5 %reduce-scatter.15.cloned.1.call-start = ((), (), s32[]{:S(2)}) async-start(), calls=%async_computation.13 | async-start | bytes 3276800 | tf_op jit(solution)/shard_map/reduce_scatter | solution.py:157
  470.4 114.4 %all-gather.20.cloned.1.call-start = ((), (), s32[]{:S(2)}) async-start(), calls=%async_computation.14 | async-start | bytes 3276800 | tf_op jit(solution)/shard_map/all_gather | solution.py:242
  530.3 162.3 %all-reduce.5.cloned.1.call-start = ((), (), s32[]{:S(2)}) async-start(), calls=%async_computation.16 | async-start | bytes 352256
  531.7 56.4 %copy-start.78 = (f32[5440]{0:T(1024)}, f32[5440]{0:T(1024)S(1)}, u32[]{:S(2)}) copy-start(f32[5440]{0:T(1024)S(1)} %constant_dynamic-update-slice_fusion.1) | copy-start | bytes 65284
  589.2 10.7 %slice-start = ((s8[10485760]{0:T(1024)(128)(4,1)}), s8[4194304]{0:T(1024)(128)(4,1)S(1)}, s32[]{:S(2)}) async-start(s8[10485760]{0:T(1024)(128)(4,1)} %bitcast.99), calls=%async_computation.19 | async-start | bytes 8388608
  589.2 10.7 %slice-start.1 = ((s8[10485760]{0:T(1024)(128)(4,1)}), s8[4194304]{0:T(1024)(128)(4,1)S(1)}, s32[]{:S(2)}) async-start(s8[10485760]{0:T(1024)(128)(4,1)} %bitcast.99), calls=%async_computation.20 | async-start | bytes 8388608
  615.3 11.3 %slice-start.3 = ((s8[5242880]{0:T(1024)(128)(4,1)}), s8[4194304]{0:T(1024)(128)(4,1)S(1)}, s32[]{:S(2)}) async-start(s8[5242880]{0:T(1024)(128)(4,1)} %bitcast.101), calls=%async_computation.22 | async-start | bytes 8388608
  633.5 102.2 %reduce-scatter.19.cloned.1.call-start = ((), (), s32[]{:S(2)}) async-start(), calls=%async_computation.17 | async-start | bytes 3686400
  650.6 139.6 %reduce-scatter.17.cloned.1.call-start = ((), (), s32[]{:S(2)}) async-start(), calls=%async_computation.15 | async-start | bytes 3276800 | tf_op jit(solution)/shard_map/reduce_scatter | solution.py:268
  659.5 212.5 %reduce-scatter.21.cloned.1.call-start = ((), (), s32[]{:S(2)}) async-start(), calls=%async_computation.18 | async-start | bytes 11059200
  659.8 10.3 %slice-start.5 = ((s8[5242880]{0:T(1024)(128)(4,1)}), s8[4194304]{0:T(1024)(128)(4,1)S(1)}, s32[]{:S(2)}) async-start(s8[5242880]{0:T(1024)(128)(4,1)} %bitcast.130), calls=%async_computation.24 | async-start | bytes 8388608
  737.1 53.1 %copy-start.13 = (f32[256,1280]{1,0:T(8,128)S(1)}, f32[256,1280]{1,0:T(8,128)}, u32[]{:S(2)}) copy-start(f32[256,1280]{1,0:T(8,128)} %copy-done.12) | copy-start | bytes 3932164
  (88 other events, 281.5 us)
Sparse Core Ops, SparseCore 0:
  9.6 57.4 all-gather.11
  69.5 31.4 all-gather.9
  138.5 52.2 reduce-scatter.10
  195.3 54.2 all-gather.13
  251.4 59.1 all-gather.15
  329.2 52.2 reduce-scatter.12
  390.2 54.2 all-gather.17
  470.5 51.0 reduce-scatter.14
  530.4 54.2 all-gather.19
  633.7 51.7 all-reduce.4
  688.9 46.7 reduce-scatter.18
  737.9 52.2 reduce-scatter.16
  793.8 78.1 reduce-scatter.20

commit v2 on v1

--- a/solution.py
+++ b/solution.py
@@ -1,6 +1,10 @@
+import functools
+
 import jax
 import jax.numpy as jnp
 from jax import lax
+from jax.experimental import pallas as pl
+from jax.experimental.pallas import tpu as pltpu
 from jax.sharding import PartitionSpec as P
 
 HEAD_DIM = 64
@@ -8,6 +12,505 @@
 
 HIGH = lax.Precision.HIGHEST
 EPS = 1e-06
+
+
+MESH_ID = pl.DeviceIdType.MESH
+ANY = pl.BlockSpec(memory_space=pl.ANY)
+IN_VMEM = pl.BlockSpec(memory_space=pltpu.VMEM)
+
+
+def remote(src, dst, send, recv, target):
+    return pltpu.make_async_remote_copy(
+        src_ref=src, dst_ref=dst, send_sem=send, recv_sem=recv,
+        device_id=target, device_id_type=MESH_ID,
+    )
+
+
+def meet(partners):
+    barrier = pltpu.get_barrier_semaphore()
+    count = 0
+    for there, target in partners:
+        if there is True:
+            pl.semaphore_signal(barrier, inc=1, device_id=target, device_id_type=MESH_ID)
+            count = count + 1
+        else:
+            @pl.when(there)
+            def _():
+                pl.semaphore_signal(barrier, inc=1, device_id=target, device_id_type=MESH_ID)
+            count = count + there.astype(jnp.int32)
+    pl.semaphore_wait(barrier, count)
+
+
+def line_partners(me, count):
+    return [
+        (me < count - 1, {"tensor": jnp.minimum(me + 1, count - 1)}),
+        (me > 0, {"tensor": jnp.maximum(me - 1, 0)}),
+    ]
+
+
+def plane_partners():
+    dp = lax.axis_index("dp")
+    return [(True, {"dp": dp + bit * (1 - 2 * ((dp // bit) % 2))}) for bit in (1, 2, 4)]
+
+
+class LineGather:
+    def __init__(self, own, out, send, recv, count, pieces):
+        self.own, self.out, self.send, self.recv = own, out, send, recv
+        self.count, self.pieces = count, pieces
+        self.me = lax.axis_index("tensor")
+        self.rows = own.shape[0] // pieces
+
+    def hop(self, way, origin, piece, step):
+        target = {"tensor": self.me + way}
+        place = self.out.at[origin, pl.ds(piece * self.rows, self.rows)]
+        src = self.own.at[pl.ds(piece * self.rows, self.rows)] if step == 0 else place
+        side = 0 if way == 1 else 1
+        return remote(
+            src, place, self.send.at[side, step, piece], self.recv.at[side, step, piece], target
+        )
+
+    def can_send(self, way, step):
+        near = self.me + way
+        origin = self.me - way * step
+        return (near >= 0) & (near < self.count) & (origin >= 0) & (origin < self.count)
+
+    def start(self, step, piece):
+        for way in (1, -1):
+            @pl.when(self.can_send(way, step))
+            def _():
+                self.hop(way, self.me - way * step, piece, step).start()
+
+    def arrive(self, step, piece):
+        for way in (1, -1):
+            origin = self.me - way * (step + 1)
+            @pl.when((origin >= 0) & (origin < self.count))
+            def _():
+                place = self.out.at[origin, pl.ds(piece * self.rows, self.rows)]
+                side = 0 if way == 1 else 1
+                remote(
+                    place, place, self.send.at[side, step, piece],
+                    self.recv.at[side, step, piece], {"tensor": self.me - way},
+                ).wait_recv()
+
+    def finish(self):
+        for step in range(self.count - 1):
+            for piece in range(self.pieces):
+                for way in (1, -1):
+                    @pl.when(self.can_send(way, step))
+                    def _():
+                        self.hop(way, self.me - way * step, piece, step).wait_send()
+
+
+def gather_kernel(
+    count, pieces, tokens, shard, whole, full, line_send, line_recv, send, recv, local
+):
+    dp = lax.axis_index("dp")
+    flip = [dp + bit * (1 - 2 * ((dp // bit) % 2)) for bit in (1, 2, 4)]
+    core, near_x, near_y = flip
+    far = near_x + 4 * (1 - 2 * ((dp // 4) % 2))
+    half = shard.shape[0] // 2
+    meet(line_partners(lax.axis_index("tensor"), count) + plane_partners())
+    line = LineGather(tokens, whole, line_send, line_recv, count, pieces)
+
+    def part(origin, which):
+        return full.at[origin, pl.ds(which * half, half)]
+
+    def flow(slot, src, origin, which, target):
+        return remote(src, part(origin, which), send.at[slot], recv.at[slot], {"dp": target})
+
+    mine = [shard.at[pl.ds(which * half, half)] for which in (0, 1)]
+    for piece in range(pieces):
+        line.start(0, piece)
+    started = []
+
+    def go(slot, src, origin, which, target):
+        copy = flow(slot, src, origin, which, target)
+        copy.start()
+        started.append(copy)
+
+    def got(slot, origin, which):
+        place = part(origin, which)
+        remote(place, place, send.at[slot], recv.at[slot], {"dp": core}).wait_recv()
+
+    go(0, mine[0], dp, 0, near_x)
+    go(2, mine[1], dp, 1, near_y)
+    go(1, mine[1], dp, 1, near_x)
+    go(3, mine[0], dp, 0, near_y)
+    go(6, mine[0], dp, 0, core)
+    go(7, mine[1], dp, 1, core)
+    keep = [
+        pltpu.make_async_copy(shard, full.at[dp], local.at[0]),
+        pltpu.make_async_copy(tokens, whole.at[line.me], local.at[1]),
+    ]
+    for copy in keep:
+        copy.start()
+    for piece in range(pieces):
+        line.arrive(0, piece)
+        line.start(1, piece)
+    got(0, near_x, 0)
+    go(4, part(near_x, 0), near_x, 0, near_y)
+    go(8, part(near_x, 0), near_x, 0, core)
+    got(2, near_y, 1)
+    go(5, part(near_y, 1), near_y, 1, near_x)
+    go(9, part(near_y, 1), near_y, 1, core)
+    for step in range(1, count - 1):
+        for piece in range(pieces):
+            line.arrive(step, piece)
+            if step + 1 < count - 1:
+                line.start(step + 1, piece)
+    got(1, near_x, 1)
+    go(10, part(near_x, 1), near_x, 1, core)
+    got(3, near_y, 0)
+    go(11, part(near_y, 0), near_y, 0, core)
+    got(4, far, 0)
+    go(12, part(far, 0), far, 0, core)
+    got(5, far, 1)
+    go(13, part(far, 1), far, 1, core)
+    def other(index):
+        return index + 1 - 2 * (index % 2)
+    for slot, origin, which in (
+        (6, core, 0), (7, core, 1), (8, other(near_x), 0), (9, other(near_y), 1),
+        (10, other(near_x), 1), (11, other(near_y), 0), (12, other(far), 0), (13, other(far), 1),
+    ):
+        got(slot, origin, which)
+    for copy in started:
+        copy.wait_send()
+    line.finish()
+    for copy in keep:
+        copy.wait()
+
+
+def gather_all(tokens, shard, count, size, pieces=2):
+    return pl.pallas_call(
+        functools.partial(gather_kernel, count, pieces),
+        out_shape=(
+            jax.ShapeDtypeStruct((count,) + tokens.shape, tokens.dtype),
+            jax.ShapeDtypeStruct((size,) + shard.shape, shard.dtype),
+        ),
+        in_specs=[IN_VMEM, IN_VMEM],
+        out_specs=(ANY, ANY),
+        scratch_shapes=[
+            pltpu.SemaphoreType.DMA((2, count - 1, pieces)),
+            pltpu.SemaphoreType.DMA((2, count - 1, pieces)),
+            pltpu.SemaphoreType.DMA((14,)),
+            pltpu.SemaphoreType.DMA((14,)),
+            pltpu.SemaphoreType.DMA((2,)),
+        ],
+        compiler_params=pltpu.CompilerParams(collective_id=1, has_side_effects=True),
+        name="gather_all",
+    )(tokens, shard)
+
+
+def everyone(count, size):
+    me, dp = lax.axis_index("tensor"), lax.axis_index("dp")
+    return [(True, {"tensor": lax.rem(me + k, count)}) for k in range(1, count)] + [
+        (True, {"dp": lax.rem(dp + k, size)}) for k in range(1, size)
+    ]
+
+
+def add_rows(dst, left, right, rows):
+    step = 16
+    def body(index, carry):
+        at = pl.ds(pl.multiple_of(index * step, step), step)
+        total = left[at, :].astype(jnp.float32) + right[at, :].astype(jnp.float32)
+        dst[at, :] = total.astype(dst.dtype)
+        return carry
+    lax.fori_loop(0, rows // step, body, 0)
+
+
+class LineScatter:
+    def __init__(self, parts, inbox, outbox, send, recv, count, pieces):
+        self.parts, self.inbox, self.outbox = parts, inbox, outbox
+        self.send, self.recv = send, recv
+        self.count, self.pieces = count, pieces
+        self.me = lax.axis_index("tensor")
+        self.rows = parts.shape[1] // pieces
+
+    def at(self, piece):
+        return pl.ds(piece * self.rows, self.rows)
+
+    def copy(self, way, src, dest, piece):
+        side = 0 if way == 1 else 1
+        return remote(
+            src, self.inbox.at[side, dest, self.at(piece)],
+            self.send.at[side, dest, piece], self.recv.at[side, dest, piece],
+            {"tensor": self.me + way},
+        )
+
+    def hops(self, way):
+        return self.me if way == 1 else self.count - 1 - self.me
+
+    def begin(self):
+        for turn in range(self.count - 1):
+            for piece in range(self.pieces):
+                for way in (1, -1):
+                    dest = self.count - 1 - turn if way == 1 else turn
+                    @pl.when(self.hops(way) == 0)
+                    def _():
+                        self.copy(way, self.parts.at[dest, self.at(piece)], dest, piece).start()
+
+    def relay(self, time, piece):
+        for way in (1, -1):
+            side = 0 if way == 1 else 1
+            turn = time - self.hops(way)
+            dest = self.count - 1 - turn if way == 1 else turn
+            beyond = dest > self.me if way == 1 else dest < self.me
+            @pl.when((self.hops(way) > 0) & (turn >= 0) & beyond)
+            def _():
+                rows = self.at(piece)
+                src = self.outbox.at[side, dest, rows]
+                self.copy(way, src, dest, piece).wait_recv()
+                add_rows(
+                    src, self.parts.at[dest, rows], self.inbox.at[side, dest, rows], self.rows
+                )
+                self.copy(way, src, dest, piece).start()
+
+    def take(self, total):
+        step = 16
+        def first(index, carry):
+            at = pl.ds(pl.multiple_of(index * step, step), step)
+            total[at, :] = self.parts[self.me, at, :].astype(jnp.float32)
+            return carry
+        lax.fori_loop(0, self.parts.shape[1] // step, first, 0)
+        for piece in range(self.pieces):
+            for way in (1, -1):
+                side = 0 if way == 1 else 1
+                @pl.when(self.hops(way) > 0)
+                def _():
+                    rows = self.at(piece)
+                    self.copy(way, self.inbox.at[side, self.me, rows], self.me, piece).wait_recv()
+                    add_rows(
+                        total.at[rows], total.at[rows], self.inbox.at[side, self.me, rows],
+                        self.rows,
+                    )
+
+    def finish(self):
+        for turn in range(self.count - 1):
+            for piece in range(self.pieces):
+                for way in (1, -1):
+                    dest = self.count - 1 - turn if way == 1 else turn
+                    sent = dest > self.me if way == 1 else dest < self.me
+                    @pl.when(sent)
+                    def _():
+                        self.copy(
+                            way, self.outbox.at[0 if way == 1 else 1, dest, self.at(piece)],
+                            dest, piece,
+                        ).wait_send()
+
+
+def line_boxes(count, rows, cols, pieces):
+    return [
+        pltpu.VMEM((2, count, rows, cols), jnp.bfloat16),
+        pltpu.VMEM((2, count, rows, cols), jnp.bfloat16),
+        pltpu.SemaphoreType.DMA((2, count, pieces)),
+        pltpu.SemaphoreType.DMA((2, count, pieces)),
+    ]
+
+
+def line_gather_kernel(count, pieces, own, whole, send, recv, local):
+    meet(line_partners(lax.axis_index("tensor"), count))
+    line = LineGather(own, whole, send, recv, count, pieces)
+    for piece in range(pieces):
+        line.start(0, piece)
+    keep = pltpu.make_async_copy(own, whole.at[line.me], local.at[0])
+    keep.start()
+    for step in range(count - 1):
+        for piece in range(pieces):
+            line.arrive(step, piece)
+            if step + 1 < count - 1:
+                line.start(step + 1, piece)
+    line.finish()
+    keep.wait()
+
+
+def line_gather(own, count, ident, pieces=4):
+    return pl.pallas_call(
+        functools.partial(line_gather_kernel, count, pieces),
+        out_shape=jax.ShapeDtypeStruct((count,) + own.shape, own.dtype),
+        in_specs=[IN_VMEM],
+        out_specs=IN_VMEM,
+        scratch_shapes=[
+            pltpu.SemaphoreType.DMA((2, count - 1, pieces)),
+            pltpu.SemaphoreType.DMA((2, count - 1, pieces)),
+            pltpu.SemaphoreType.DMA((1,)),
+        ],
+        compiler_params=pltpu.CompilerParams(collective_id=ident, has_side_effects=True),
+        name=f"line_gather_{ident}",
+    )(own).reshape(count * own.shape[0], own.shape[1])
+
+
+def line_scatter_kernel(count, pieces, parts, total, inbox, outbox, send, recv):
+    meet(line_partners(lax.axis_index("tensor"), count))
+    line = LineScatter(parts, inbox, outbox, send, recv, count, pieces)
+    line.begin()
+    for time in range(1, count - 1):
+        for piece in range(pieces):
+            line.relay(time, piece)
+    line.take(total)
+    line.finish()
+
+
+def line_scatter(value, count, ident, pieces=4):
+    rows, cols = value.shape[0] // count, value.shape[1]
+    return pl.pallas_call(
+        functools.partial(line_scatter_kernel, count, pieces),
+        out_shape=jax.ShapeDtypeStruct((rows, cols), jnp.float32),
+        in_specs=[IN_VMEM],
+        out_specs=IN_VMEM,
+        scratch_shapes=line_boxes(count, rows, cols, pieces),
+        compiler_params=pltpu.CompilerParams(collective_id=ident, has_side_effects=True),
+        name=f"line_scatter_{ident}",
+    )(value.astype(jnp.bfloat16).reshape(count, rows, cols))
+
+
+def scatter_kernel(
+    count, size, pieces, parts, grads, small, total, mine, summed,
+    inbox, outbox, line_send, line_recv,
+    pair_in, held, far_in, near_in, send, recv,
+    small_dp, small_line, partial, small_send, small_recv,
+):
+    me, dp = lax.axis_index("tensor"), lax.axis_index("dp")
+    core, near_x, near_y = [dp + bit * (1 - 2 * ((dp // bit) % 2)) for bit in (1, 2, 4)]
+    far = near_x + 4 * (1 - 2 * ((dp // 4) % 2))
+    half = grads.shape[1] // 2
+    halves = [pl.ds(0, half), pl.ds(half, half)]
+    meet(everyone(count, size))
+    line = LineScatter(parts, inbox, outbox, line_send, line_recv, count, pieces)
+    line.begin()
+    order = (far, near_x, near_y, dp)
+    pair = [
+        remote(
+            grads.at[dest + 1 - 2 * (dest % 2)], pair_in.at[k], send.at[k], recv.at[k],
+            {"dp": core},
+        )
+        for k, dest in enumerate(order)
+    ]
+    for copy in pair:
+        copy.start()
+    small_copies = [
+        remote(small, small_dp.at[k - 1], small_send.at[k - 1], small_recv.at[k - 1],
+               {"dp": lax.rem(dp + k, size)})
+        for k in range(1, size)
+    ]
+    for copy in small_copies:
+        copy.start()
+
+    def ready(k, which):
+        rows = halves[which]
+        add_rows(held.at[k, rows], grads.at[order[k], rows], pair_in.at[k, rows], half)
+
+    def flow(slot, src, dst, target):
+        return remote(src, dst, send.at[slot], recv.at[slot], {"dp": target})
+
+    pair[0].wait_recv()
+    ready(0, 0)
+    far_x = flow(4, held.at[0, halves[0]], far_in.at[0], near_x)
+    far_x.start()
+    ready(0, 1)
+    far_y = flow(5, held.at[0, halves[1]], far_in.at[1], near_y)
+    far_y.start()
+    pair[1].wait_recv()
+    ready(1, 0)
+    x_low = flow(6, held.at[1, halves[0]], near_in.at[0, halves[0]], near_x)
+    x_low.start()
+    pair[2].wait_recv()
+    ready(2, 1)
+    y_high = flow(7, held.at[2, halves[1]], near_in.at[1, halves[1]], near_y)
+    y_high.start()
+    ready(1, 1)
+    ready(2, 0)
+    pair[3].wait_recv()
+    for copy in small_copies:
+        copy.wait_recv()
+    gathered = small[...]
+    for k in range(size - 1):
+        gathered = gathered + small_dp[k]
+    partial[...] = gathered
+    tiny = [
+        remote(partial, small_line.at[k - 1], small_send.at[size - 2 + k],
+               small_recv.at[size - 2 + k], {"tensor": lax.rem(me + k, count)})
+        for k in range(1, count)
+    ]
+    for copy in tiny:
+        copy.start()
+    for piece in range(pieces):
+        line.relay(1, piece)
+    far_x.wait_recv()
+    add_rows(held.at[2, halves[0]], held.at[2, halves[0]], far_in.at[0], half)
+    y_low = flow(8, held.at[2, halves[0]], near_in.at[1, halves[0]], near_y)
+    y_low.start()
+    far_y.wait_recv()
+    add_rows(held.at[1, halves[1]], held.at[1, halves[1]], far_in.at[1], half)
+    x_high = flow(9, held.at[1, halves[1]], near_in.at[0, halves[1]], near_x)
+    x_high.start()
+    for time in range(2, count - 1):
+        for piece in range(pieces):
+            line.relay(time, piece)
+    for copy in tiny:
+        copy.wait_recv()
+    every = partial[...]
+    for k in range(count - 1):
+        every = every + small_line[k]
+    summed[0] = partial[...]
+    summed[1] = every
+    line.take(total)
+    step = 16
+    def last(rows_at, near_ready):
+        for copy in near_ready:
+            copy.wait_recv()
+        def body(index, carry):
+            at = pl.ds(pl.multiple_of(rows_at + index * step, step), step)
+            mine[at, :] = (
+                grads[dp, at, :].astype(jnp.float32)
+                + pair_in[3, at, :].astype(jnp.float32)
+                + near_in[0, at, :].astype(jnp.float32)
+                + near_in[1, at, :].astype(jnp.float32)
+            )
+            return carry
+        lax.fori_loop(0, half // step, body, 0)
+    last(0, (x_low, y_low))
+    last(half, (x_high, y_high))
+    for copy in pair + small_copies + tiny + [far_x, far_y, x_low, y_high, y_low, x_high]:
+        copy.wait_send()
+    line.finish()
+
+
+def scatter_all(value, grads, small, count, size, pieces=2):
+    rows, cols = value.shape[0] // count, value.shape[1]
+    block, wide = grads.shape[0] // size, grads.shape[1]
+    low = jnp.bfloat16
+    return pl.pallas_call(
+        functools.partial(scatter_kernel, count, size, pieces),
+        out_shape=(
+            jax.ShapeDtypeStruct((rows, cols), jnp.float32),
+            jax.ShapeDtypeStruct((block, wide), jnp.float32),
+            jax.ShapeDtypeStruct((2,) + small.shape, jnp.float32),
+        ),
+        in_specs=[IN_VMEM] * 3,
+        out_specs=(IN_VMEM,) * 3,
+        scratch_shapes=line_boxes(count, rows, cols, pieces)
+        + [
+            pltpu.VMEM((4, block, wide), low),
+            pltpu.VMEM((3, block, wide), low),
+            pltpu.VMEM((2, block // 2, wide), low),
+            pltpu.VMEM((2, block, wide), low),
+            pltpu.SemaphoreType.DMA((10,)),
+            pltpu.SemaphoreType.DMA((10,)),
+            pltpu.VMEM((size - 1,) + small.shape, jnp.float32),
+            pltpu.VMEM((count - 1,) + small.shape, jnp.float32),
+            pltpu.VMEM(small.shape, jnp.float32),
+            pltpu.SemaphoreType.DMA((size + count - 2,)),
+            pltpu.SemaphoreType.DMA((size + count - 2,)),
+        ],
+        compiler_params=pltpu.CompilerParams(
+            collective_id=2, has_side_effects=True, vmem_limit_bytes=62 * 1024 * 1024
+        ),
+        name="scatter_all",
+    )(
+        value.astype(low).reshape(count, rows, cols),
+        grads.astype(low).reshape(size, block, wide),
+        small,
+    )
 
 
 def unit_rows(value):
@@ -175,15 +678,21 @@
     alpha_mlp,
     cotangent,
 ):
-    attn_w = lax.all_gather(
-        jnp.concatenate([w_query, w_key, w_value, w_out], axis=1), "dp", axis=0, tiled=True
-    )
-    query_w, key_w, value_w, out_w = jnp.split(attn_w, 4, axis=1)
-    whole = lax.all_gather(tokens, "tensor", axis=0, tiled=True)
-    mlp_w = lax.all_gather(
-        jnp.concatenate([w_up, w_gate, w_down], axis=1), "dp", axis=0, tiled=True
-    )
-    up_w, gate_w, down_w = jnp.split(mlp_w, 3, axis=1)
+    count, size = lax.axis_size("tensor"), lax.axis_size("dp")
+    shard = jnp.concatenate([w_query, w_key, w_value, w_out, w_up, w_gate, w_down], axis=1)
+    if size == 8:
+        whole, weights = gather_all(tokens, shard, count, size)
+        whole = whole.reshape(count * tokens.shape[0], tokens.shape[1])
+        weights = weights.reshape(size * shard.shape[0], shard.shape[1])
+    else:
+        whole = line_gather(tokens, count, 1)
+        weights = lax.all_gather(shard, "dp", axis=0, tiled=True)
+    heads, units = w_query.shape[1], w_up.shape[1]
+    query_w, key_w, value_w, out_w, up_w, gate_w, down_w = jnp.split(
+        weights,
+        (heads, 2 * heads, 3 * heads, 4 * heads, 4 * heads + units, 4 * heads + 2 * units),
+        axis=1,
+    )
     length = whole.shape[0]
     width = query_w.shape[1]
     block = min(512, length)
@@ -201,26 +710,26 @@
     value3 = value_low.reshape(shape3)
     attended, totals = attend(query3, key3, value3, block)
     attended_low = attended.reshape(length, width).astype(jnp.bfloat16)
-    attn_sum = scatter_low(contract_cols(attended_low, out_w), "tensor")
+    attn_sum = line_scatter(contract_cols(attended_low, out_w), count, 4)
     attn_unit, attn_norm = unit_rows(attn_sum)
     residual = tokens.astype(jnp.float32)
     mid, mid_norm = unit_rows(residual + alpha_attn * (attn_unit - residual))
     mid_low = mid.astype(jnp.bfloat16)
-    mid_whole = lax.all_gather(mid_low, "tensor", axis=0, tiled=True)
+    mid_whole = line_gather(mid_low, count, 3)
     up_sum = jnp.dot(mid_whole, up_w, preferred_element_type=jnp.float32)
     gate_sum = jnp.dot(mid_whole, gate_w, preferred_element_type=jnp.float32)
     up_val = up_sum * up_scale
     gate_val = gate_sum * gate_scale
     sigma = jax.nn.sigmoid(gate_val)
     hidden_low = (up_val * (gate_val * sigma)).astype(jnp.bfloat16)
-    mlp_sum = scatter_low(contract_cols(hidden_low, down_w), "tensor")
+    mlp_sum = line_scatter(contract_cols(hidden_low, down_w), count, 7)
     mlp_unit, mlp_norm = unit_rows(mlp_sum)
     final, final_norm = unit_rows(mid + alpha_mlp * (mlp_unit - mid))
     output = final.astype(jnp.bfloat16)
     g_second = unit_back(cotangent.astype(jnp.float32), final, final_norm)
     g_alpha_mlp = jnp.sum((mlp_unit - mid) * g_second, axis=0)
     g_mlp_low = unit_back(alpha_mlp * g_second, mlp_unit, mlp_norm).astype(jnp.bfloat16)
-    g_mlp_whole = lax.all_gather(g_mlp_low, "tensor", axis=0, tiled=True)
+    g_mlp_whole = line_gather(g_mlp_low, count, 5)
     down_grad = contract_rows(g_mlp_whole, hidden_low)
     g_hidden = jnp.dot(g_mlp_whole, down_w, preferred_element_type=jnp.float32)
     g_up = g_hidden * (gate_val * sigma)
@@ -232,14 +741,11 @@
     up_grad = contract_rows(mid_whole, g_up_low)
     gate_grad = contract_rows(mid_whole, g_gate_low)
     g_mid_part = contract_cols(g_up_low, up_w) + contract_cols(g_gate_low, gate_w)
-    g_mid = (1.0 - alpha_mlp) * g_second + scatter_low(g_mid_part, "tensor")
-    up_grad, gate_grad, down_grad = jnp.split(
-        scatter_low(jnp.concatenate([up_grad, gate_grad, down_grad], axis=1), "dp"), 3, axis=1
-    )
+    g_mid = (1.0 - alpha_mlp) * g_second + line_scatter(g_mid_part, count, 8)
     g_first = unit_back(g_mid, mid, mid_norm)
     g_alpha_attn = jnp.sum((attn_unit - residual) * g_first, axis=0)
     g_attn_low = unit_back(alpha_attn * g_first, attn_unit, attn_norm).astype(jnp.bfloat16)
-    g_attn_whole = lax.all_gather(g_attn_low, "tensor", axis=0, tiled=True)
+    g_attn_whole = line_gather(g_attn_low, count, 6)
     out_grad = contract_rows(g_attn_whole, attended_low)
     g_attended_low = jnp.dot(g_attn_whole, out_w, preferred_element_type=jnp.float32).astype(
         jnp.bfloat16
@@ -265,30 +771,30 @@
         + contract_cols(g_k_raw_low, key_w)
         + contract_cols(g_value_low, value_w)
     )
-    tokens_grad = (1.0 - alpha_attn) * g_first + lax.psum_scatter(
-        g_tok_part.astype(jnp.bfloat16), "tensor", scatter_dimension=0, tiled=True
-    ).astype(jnp.float32)
-    query_grad, key_grad, value_grad, out_grad = jnp.split(
-        scatter_low(
-            jnp.concatenate([query_grad, key_grad, value_grad, out_grad], axis=1), "dp"
-        ),
-        4,
+    grads = jnp.concatenate(
+        [query_grad, key_grad, value_grad, out_grad, up_grad, gate_grad, down_grad], axis=1
+    )
+    model = g_alpha_attn.shape[0]
+    vectors = (g_alpha_attn, g_alpha_mlp, up_scale_grad, gate_scale_grad, qk_grad)
+    packed = jnp.concatenate(vectors)
+    packed = jnp.pad(packed, (0, 8 * model - packed.shape[0])).reshape(8, model)
+    if size == 8:
+        g_tokens, mine, sums = scatter_all(g_tok_part, grads, packed, count, size)
+    else:
+        g_tokens = line_scatter(g_tok_part, count, 2)
+        mine = scatter_low(grads, "dp")
+        within = lax.psum(packed, "dp")
+        sums = jnp.stack([within, lax.psum(within, "tensor")])
+    tokens_grad = (1.0 - alpha_attn) * g_first + g_tokens
+    query_grad, key_grad, value_grad, out_grad, up_grad, gate_grad, down_grad = jnp.split(
+        mine,
+        (heads, 2 * heads, 3 * heads, 4 * heads, 4 * heads + units, 4 * heads + 2 * units),
         axis=1,
     )
-    sizes = (g_alpha_attn.shape[0], g_alpha_mlp.shape[0], up_scale_grad.shape[0], gate_scale_grad.shape[0])
-    cuts = (sizes[0], sizes[0] + sizes[1], sum(sizes[:3]), sum(sizes))
-    small = jnp.sum(
-        lax.all_gather(
-            jnp.concatenate([g_alpha_attn, g_alpha_mlp, up_scale_grad, gate_scale_grad, qk_grad]),
-            "dp",
-        ),
-        axis=0,
-    )
-    alphas = jnp.sum(lax.all_gather(small[: cuts[1]], "tensor"), axis=0)
-    g_alpha_attn, g_alpha_mlp = alphas[: cuts[0]], alphas[cuts[0] :]
-    up_scale_grad = small[cuts[1] : cuts[2]]
-    gate_scale_grad = small[cuts[2] : cuts[3]]
-    qk_grad = small[cuts[3] :]
+    g_alpha_attn, g_alpha_mlp = sums[1, 0], sums[1, 1]
+    flat = sums[0].reshape(8 * model)[2 * model :]
+    up_scale_grad, gate_scale_grad = flat[:units], flat[units : 2 * units]
+    qk_grad = flat[2 * units : 2 * units + heads]
     return (
         output,
         tokens_grad,

time: 893 us -> 681 us (0.76)
  waiting for transfers between devices: 622 us -> 0 us
  Pallas kernels: 0 us -> 411 us
  matrix products: 124 us -> 157 us
  between operations: 16.4 us -> 2.03 us
  blocking collectives: 13.1 us -> 0 us
  other arithmetic: 57.6 us -> 45.6 us
    pallas_call x0 -> x8, Pallas kernels: none -> 411 us  [the longest x3 143 us: line_gather(): pl.pallas_call(functools.partial(line_gather_kernel, count, pieces), out_...]
    all_gather x6 -> x0, waiting for transfers between devices: 310 us -> none  [the longest x1 60.9 us: on_device(): lax.all_gather(jnp.concatenate([w_up, w_gate, w_down], axis=1), 'dp', axi...]
    reduce_scatter x4 -> x0, waiting for transfers between devices: 204 us -> none  [the longest x3 155 us: scatter_low(): lax.psum_scatter(value.astype(jnp.bfloat16), axis, scatter_dimension=0, t...]
    unnamed x16 -> x0, waiting for transfers between devices: 108 us -> none
    unnamed x233 -> x162, local copies, waits for them, and re-layouts: 41 us -> 6.64 us
    concatenate x1 -> x2, local copies, waits for them, and re-layouts: 2.03 us -> 24.1 us  [the longest x1 20.2 us: on_device(): jnp.concatenate([query_grad, key_grad, value_grad, out_grad, up_grad, gat...]
    dot_general x0 -> x4, local copies, waits for them, and re-layouts: none -> 18.5 us  [contract_rows(): lax.dot_general(left, right, (((0,), (0,)), ((), ())), preferred_element_...]
    all_gather x1 -> x0, blocking collectives: 13.1 us -> none  [on_device(): alphas = jnp.sum(lax.all_gather(small[:cuts[1]], 'tensor'), axis=0)]
  transfers between devices with their start and end apart: 13 -> 0, of which waited for: 12 -> 0; matrix products, arithmetic and copies ran while one was open for 8% -> 0% of each run, Pallas kernels for 0% -> 0%
where the time goes in v2:
time: 681 us; the launch traced here: 675 us
  Pallas kernels  411 us (60%)
  matrix products  157 us (23%)
  local copies, waits for them, and re-layouts  59.5 us (9%)
  other arithmetic  45.6 us (7%)
    pallas_call x3, Pallas kernels, line_gather(): pl.pallas_call(functools.partial(line_gather_kernel, count, pieces), out_...  143 us
    pallas_call x3, Pallas kernels, line_scatter(): pl.pallas_call(functools.partial(line_scatter_kernel, count, pieces), out...  136 us
    pallas_call x1, Pallas kernels, scatter_all(): pl.pallas_call(functools.partial(scatter_kernel, count, size, pieces), ou...  69.4 us
    pallas_call x1, Pallas kernels, gather_all(): pl.pallas_call(functools.partial(gather_kernel, count, pieces), out_shape...  63.3 us
    dot_general x7, matrix products, contract_cols(): lax.dot_general(left, right, (((1,), (1,)), ((), ())), preferred_element_...  34.5 us
    dot_general x7, matrix products, contract_rows(): lax.dot_general(left, right, (((0,), (0,)), ((), ())), preferred_element_...  30.1 us
    concatenate x1, local copies, waits for them, and re-layouts, on_device(): jnp.concatenate([query_grad, key_grad, value_grad, out_grad, up_grad, gat...  20.2 us
    dot_general x4, local copies, waits for them, and re-layouts, contract_rows(): lax.dot_general(left, right, (((0,), (0,)), ((), ())), preferred_element_...  18.5 us

profile of v2, /device:TPU:0, one launch (start us, length us, event | category | flops | bytes accessed | tf_op | source)
XLA Modules:
  0.0 675.4 jit_solution(6163184528077258679)
XLA Ops:
  8.7 63.3 %gather_all.1 = (bf16[4,256,1280]{2,1,0:T(8,128)(2,1)}, bf16[8,160,5120]{2,1,0:T(8,128)(2,1)}) custom-call(bf16[256,1280]{1,0:T(8,128)(2,1)} %tokens.1, bf16[160,5120]{1,0:T(8,128)(2,1)} %concatenate.60.shard), custom_call_target="tpu_custom_call" | custom-call | tf_op jit(solution)/shard_map/gather_all/pallas_call | solution.py:184
  81.8 4.7 copy.40
  87.5 6.3 fusion.33
  114.6 4.6 convolution_convert_fusion.4
  119.1 47.7 %line_scatter_4.1 = f32[256,1280]{1,0:T(8,128)} custom-call(bf16[4,256,1280]{2,1,0:T(8,128)(2,1)} %bitcast.160), custom_call_target="tpu_custom_call" | custom-call | tf_op jit(solution)/shard_map/line_scatter_4/pallas_call | solution.py:355
  171.1 49.4 %line_gather_3.1 = bf16[4,256,1280]{2,1,0:T(8,128)(2,1)} custom-call(bf16[256,1280]{1,0:T(8,128)(2,1)} %multiply_convert_fusion.10.own), custom_call_target="tpu_custom_call" | custom-call | tf_op jit(solution)/shard_map/line_gather_3/pallas_call | solution.py:327
  220.5 4.5 copy.42
  225.0 6.4 fusion.8
  231.5 9.5 %multiply_convert_fusion.4 = (bf16[1024,1280]{1,0:T(8,128)(2,1)S(1)}, f32[1024,1280]{1,0:T(8,128)}) fusion(f32[1280]{0:T(1024)S(1)} %copy-done.64, f32[1024,1280]{1,0:T(8,128)S(1)} %fusion.8, f32[1280]{0:T(1024)S(1)} %copy-done.65, bf16[1024,1280]{1,0:T(8,128)(2,1)S(1)} %bitcast.139, bf16[1280,5120]{1,0:T(8,128)(2,1)} %bitcast.175), kind=kOutput, calls=%fused_computation.16 | convolution fusion | flops 3365928960 | bytes 19015680 | tf_op jit(solution)/shard_map/dot_general | solution.py:719
  241.0 7.8 %convolution_convert_fusion.3 = bf16[1024,1280]{1,0:T(8,128)(2,1)} fusion(bf16[1024,1280]{1,0:T(8,128)(2,1)S(1)} %get-tuple-element.151, bf16[1280,5120]{1,0:T(8,128)(2,1)} %bitcast.176), kind=kOutput, calls=%fused_computation.26 | convolution fusion | flops 3356753920 | bytes 8519680 | tf_op jit(solution)/shard_map/dot_general | solution.py:532
  248.8 44.6 %line_scatter_7.1 = f32[256,1280]{1,0:T(8,128)} custom-call(bf16[4,256,1280]{2,1,0:T(8,128)(2,1)} %bitcast.161), custom_call_target="tpu_custom_call" | custom-call | tf_op jit(solution)/shard_map/line_scatter_7/pallas_call | solution.py:355
  300.0 46.8 %line_gather_5.1 = bf16[4,256,1280]{2,1,0:T(8,128)(2,1)} custom-call(bf16[256,1280]{1,0:T(8,128)(2,1)} %multiply_convert_fusion.6.own), custom_call_target="tpu_custom_call" | custom-call | tf_op jit(solution)/shard_map/line_gather_5/pallas_call | solution.py:327
  346.8 13.0 %multiply_reduce_fusion.1 = (f32[1280]{0:T(1024)S(1)}, f32[1280]{0:T(1024)S(1)}, f32[1024,1280]{1,0:T(8,128)}, bf16[1024,1280]{1,0:T(8,128)(2,1)}) fusion(f32[1024,1280]{1,0:T(8,128)} %copy-done.67, f32[1024,1280]{1,0:T(8,128)} %get-tuple-element.152, f32[1280]{0:T(1024)S(1)} %copy-done.65, f32[1280]{0:T(1024)S(1)} %copy-done.64, ...), kind=kOutput, calls=%fused_computation.7 | convolution fusion | flops 3380344320 | bytes 24268800 | tf_op jit(solution)/shard_map/dot_general | solution.py:734
  359.8 4.5 copy.43
  364.2 8.0 %convolution_convert_fusion = bf16[8,160,1280]{2,1,0:T(8,128)(2,1)} fusion(bf16[8,160,1024]{2,1,0:T(8,128)(2,1)} %bitcast.158, bf16[1024,1280]{1,0:T(8,128)(2,1)} %copy-done.69), kind=kOutput, calls=%fused_computation.22 | convolution fusion | flops 3357081600 | bytes 8519680 | tf_op jit(solution)/shard_map/dot_general | solution.py:526
  372.3 5.0 convolution_convert_fusion.1
  377.3 4.9 convolution_convert_fusion.2
  382.3 5.3 fusion.10
  387.5 6.6 add_convert_fusion.1
  394.2 43.4 %line_scatter_8.1 = f32[256,1280]{1,0:T(8,128)} custom-call(bf16[4,256,1280]{2,1,0:T(8,128)(2,1)} %bitcast.159), custom_call_target="tpu_custom_call" | custom-call | tf_op jit(solution)/shard_map/line_scatter_8/pallas_call | solution.py:355
  443.0 46.6 %line_gather_6.1 = bf16[4,256,1280]{2,1,0:T(8,128)(2,1)} custom-call(bf16[256,1280]{1,0:T(8,128)(2,1)} %multiply_convert_fusion.5.own), custom_call_target="tpu_custom_call" | custom-call | tf_op jit(solution)/shard_map/line_gather_6/pallas_call | solution.py:327
  493.1 4.0 convolution_bitcast_fusion.1
  497.2 5.8 fusion.25
  505.6 4.9 copy.41
  510.6 4.5 convolution_convert_fusion.5
  515.1 6.6 multiply_reduce_fusion.3
  521.8 4.2 multiply_convert_fusion.1
  547.2 7.2 %fusion.48 = (f32[1024,320]{0,1:T(8,128)S(1)}, f32[1024,320]{0,1:T(8,128)S(1)}, f32[1024,320]{0,1:T(8,128)S(1)}) fusion(f32[320]{0:T(512)S(1)} %copy-done.60, f32[1024,320]{0,1:T(8,128)S(1)} %fusion.22, f32[1024,320]{0,1:T(8,128)S(1)} %copy-done.19, f32[1024,320]{0,1:T(8,128)S(1)} %copy-done.8, f32[1024,5]{1,0:T(8,128)S(1)} %fusion.74, ...), kind=kOutput, calls=%fused_computation.114 | convolution fusion | flops 21957760 | bytes 9200960 | tf_op jit(solution)/shard_map/dot_general | solution.py:586
  555.5 5.6 fusion.37
  566.1 20.2 %concatenate.74.grads = bf16[8,160,5120]{2,1,0:T(8,128)(2,1)} concatenate(bf16[8,160,320]{2,1,0:T(8,128)(2,1)} %convolution_convert_fusion.8, bf16[8,160,320]{2,1,0:T(8,128)(2,1)} %convolution_convert_fusion.7, bf16[8,160,320]{2,1,0:T(8,128)(2,1)S(1)} %copy-done.38, bf16[8,160,320]{2,1,0:T(8,128)(2,1)S(1)} %copy-done.39, bf16[8,160,1280]{2,1,0:T(8,128)(2,1)} %convolution_convert_fusion.2, ...), dimensions={2} | concatenate | bytes 26214400 | tf_op jit(solution)/shard_map/concatenate | solution.py:774
  592.2 4.3 add_convert_fusion
  596.5 69.4 %scatter_all.1 = (f32[256,1280]{1,0:T(8,128)}, f32[160,5120]{1,0:T(8,128)}, f32[2,8,1280]{2,1,0:T(8,128)}) custom-call(bf16[4,256,1280]{2,1,0:T(8,128)(2,1)} %bitcast.132, bf16[8,160,5120]{2,1,0:T(8,128)(2,1)} %concatenate.74.grads, f32[8,1280]{1,0:T(8,128)} %reshape.365.small), custom_call_target="tpu_custom_call" | custom-call | tf_op jit(solution)/shard_map/scatter_all/pallas_call | solution.py:482
  (249 shorter events, 103.7 us)
Async XLA Ops:
  2.3 95.5 %copy-start.47 = (s32[320]{0:T(512)}, s32[320]{0:T(512)S(1)}, u32[]{:S(2)}) copy-start(s32[320]{0:T(512)S(1)} %get-tuple-element.162) | copy-start | bytes 3844
  2.3 95.6 %copy-start.49 = (s32[320]{0:T(512)}, s32[320]{0:T(512)S(1)}, u32[]{:S(2)}) copy-start(s32[320]{0:T(512)S(1)} %get-tuple-element.163) | copy-start | bytes 3844
  87.5 6.4 copy-start.57
  100.8 4.9 copy-start.15
  100.9 4.9 copy-start.20
  105.7 8.8 %copy-start.45 = (bf16[5,64,512]{2,1,0:T(8,128)(2,1)}, bf16[5,64,512]{2,1,0:T(8,128)(2,1)S(1)}, u32[]{:S(2)}) copy-start(bf16[5,64,512]{2,1,0:T(8,128)(2,1)S(1)} %convolution_convert_fusion.12) | copy-start | bytes 983044
  114.5 4.7 copy-start.46
  119.1 49.2 %copy-start.17 = (bf16[256,1280]{1,0:T(8,128)(2,1)S(1)}, bf16[256,1280]{1,0:T(8,128)(2,1)}, u32[]{:S(2)}) copy-start(bf16[256,1280]{1,0:T(8,128)(2,1)} %tokens.1) | copy-start | bytes 1966084
  119.1 49.2 %copy-start.52 = (f32[1280]{0:T(1024)S(1)}, f32[1280]{0:T(1024)}, u32[]{:S(2)}) copy-start(f32[1280]{0:T(1024)} %param.37) | copy-start | bytes 15364
  225.0 6.4 copy-start.14
  225.0 6.4 copy-start.64
  225.0 6.4 copy-start.65
  231.5 9.5 %copy-start.67 = (f32[1024,1280]{1,0:T(8,128)}, f32[1024,1280]{1,0:T(8,128)S(1)}, u32[]{:S(2)}) copy-start(f32[1024,1280]{1,0:T(8,128)S(1)} %fusion.8) | copy-start | bytes 15728644
  241.0 7.8 %copy-start.69 = (bf16[1024,1280]{1,0:T(8,128)(2,1)}, bf16[1024,1280]{1,0:T(8,128)(2,1)S(1)}, u32[]{:S(2)}) copy-start(bf16[1024,1280]{1,0:T(8,128)(2,1)S(1)} %get-tuple-element.151) | copy-start | bytes 7864324
  248.8 46.2 %copy-start.51 = (f32[1280]{0:T(1024)S(1)}, f32[1280]{0:T(1024)}, u32[]{:S(2)}) copy-start(f32[1280]{0:T(1024)} %param.38) | copy-start | bytes 15364
  364.2 8.0 %copy-start.29 = (bf16[1280,1024]{1,0:T(8,128)(2,1)S(1)}, bf16[1280,1024]{1,0:T(8,128)(2,1)}, u32[]{:S(2)}) copy-start(bf16[1280,1024]{1,0:T(8,128)(2,1)} %copy.42) | copy-start | bytes 7864324
  364.2 8.0 %copy-start.66 = (f32[1024,1280]{1,0:T(8,128)S(1)}, f32[1024,1280]{1,0:T(8,128)}, u32[]{:S(2)}) copy-start(f32[1024,1280]{1,0:T(8,128)} %get-tuple-element.98) | copy-start | bytes 15728644
  372.3 5.0 copy-start.68
  372.3 9.9 %slice-start.5 = ((s8[13107200]{0:T(1024)(128)(4,1)}), s8[4194304]{0:T(1024)(128)(4,1)S(1)}, s32[]{:S(2)}) async-start(s8[13107200]{0:T(1024)(128)(4,1)} %bitcast.182), calls=%async_computation.5 | async-start | bytes 8388608
  372.3 9.9 %slice-start.6 = ((s8[13107200]{0:T(1024)(128)(4,1)}), s8[4194304]{0:T(1024)(128)(4,1)S(1)}, s32[]{:S(2)}) async-start(s8[13107200]{0:T(1024)(128)(4,1)} %bitcast.182), calls=%async_computation.6 | async-start | bytes 8388608
  377.3 5.0 slice-start.7
  377.3 5.0 slice-start.8
  497.2 5.9 copy-start.27
  505.6 16.1 %slice-start.3 = ((s8[5242880]{0:T(1024)(128)(4,1)}), s8[1048576]{0:T(1024)(128)(4,1)S(1)}, s32[]{:S(2)}) async-start(s8[5242880]{0:T(1024)(128)(4,1)} %bitcast.124), calls=%async_computation.3 | async-start | bytes 2097152
  510.5 4.6 copy-start.35
  510.5 11.2 %slice-start.4 = ((s8[5242880]{0:T(1024)(128)(4,1)}), s8[4194304]{0:T(1024)(128)(4,1)S(1)}, s32[]{:S(2)}) async-start(s8[5242880]{0:T(1024)(128)(4,1)} %bitcast.124), calls=%async_computation.4 | async-start | bytes 8388608
  515.1 12.3 %slice-start = ((s8[10485760]{0:T(1024)(128)(4,1)}), s8[4194304]{0:T(1024)(128)(4,1)S(1)}, s32[]{:S(2)}) async-start(s8[10485760]{0:T(1024)(128)(4,1)} %bitcast.122), calls=%async_computation | async-start | bytes 8388608
  515.1 12.3 %slice-start.1 = ((s8[10485760]{0:T(1024)(128)(4,1)}), s8[4194304]{0:T(1024)(128)(4,1)S(1)}, s32[]{:S(2)}) async-start(s8[10485760]{0:T(1024)(128)(4,1)} %bitcast.122), calls=%async_computation.1 | async-start | bytes 8388608
  521.7 5.7 slice-start.2
  555.5 5.6 copy-start.28
  596.5 69.4 %copy-start.13 = (f32[256,1280]{1,0:T(8,128)S(1)}, f32[256,1280]{1,0:T(8,128)}, u32[]{:S(2)}) copy-start(f32[256,1280]{1,0:T(8,128)} %copy-done.12) | copy-start | bytes 3932164
  596.5 69.4 %copy-start.56 = (f32[1280]{0:T(1024)S(1)}, f32[1280]{0:T(1024)}, u32[]{:S(2)}) copy-start(f32[1280]{0:T(1024)} %broadcast_subtract_fusion.1) | copy-start | bytes 15364
  (47 other events, 100.4 us)

commit v3 on v2

--- a/solution.py
+++ b/solution.py
@@ -363,30 +363,189 @@
     )(value.astype(jnp.bfloat16).reshape(count, rows, cols))
 
 
+class PlaneScatter:
+    def __init__(self, grads, mine, pair_in, held, far_in, near_in, send, recv):
+        self.grads, self.mine, self.pair_in, self.held = grads, mine, pair_in, held
+        self.far_in, self.near_in, self.send, self.recv = far_in, near_in, send, recv
+        dp = lax.axis_index("dp")
+        core, near_x, near_y = [dp + bit * (1 - 2 * ((dp // bit) % 2)) for bit in (1, 2, 4)]
+        far = near_x + 4 * (1 - 2 * ((dp // 4) % 2))
+        self.order = (far, near_x, near_y, dp)
+        half = grads.shape[1] // 2
+        self.half = half
+        low, high = pl.ds(0, half), pl.ds(half, half)
+        self.halves = (low, high)
+        self.pair = [
+            remote(
+                grads.at[dest + 1 - 2 * (dest % 2)], pair_in.at[k], send.at[k], recv.at[k],
+                {"dp": core},
+            )
+            for k, dest in enumerate(self.order)
+        ]
+
+        def flow(slot, src, dst, target):
+            return remote(src, dst, send.at[slot], recv.at[slot], {"dp": target})
+
+        self.far_x = flow(4, held.at[0, low], far_in.at[0], near_x)
+        self.far_y = flow(5, held.at[0, high], far_in.at[1], near_y)
+        self.x_low = flow(6, held.at[1, low], near_in.at[0, low], near_x)
+        self.y_high = flow(7, held.at[2, high], near_in.at[1, high], near_y)
+        self.y_low = flow(8, held.at[2, low], near_in.at[1, low], near_y)
+        self.x_high = flow(9, held.at[1, high], near_in.at[0, high], near_x)
+
+    def begin(self):
+        for copy in self.pair:
+            copy.start()
+
+    def ready(self, k, which):
+        rows = self.halves[which]
+        add_rows(
+            self.held.at[k, rows], self.grads.at[self.order[k], rows],
+            self.pair_in.at[k, rows], self.half,
+        )
+
+    def outward(self):
+        self.pair[0].wait_recv()
+        self.ready(0, 0)
+        self.far_x.start()
+        self.ready(0, 1)
+        self.far_y.start()
+        self.pair[1].wait_recv()
+        self.ready(1, 0)
+        self.x_low.start()
+        self.pair[2].wait_recv()
+        self.ready(2, 1)
+        self.y_high.start()
+        self.ready(1, 1)
+        self.ready(2, 0)
+        self.pair[3].wait_recv()
+
+    def onward(self):
+        low, high = self.halves
+        self.far_x.wait_recv()
+        add_rows(self.held.at[2, low], self.held.at[2, low], self.far_in.at[0], self.half)
+        self.y_low.start()
+        self.far_y.wait_recv()
+        add_rows(self.held.at[1, high], self.held.at[1, high], self.far_in.at[1], self.half)
+        self.x_high.start()
+
+    def take(self):
+        step = 16
+        for copy in (self.x_low, self.y_low, self.x_high, self.y_high):
+            copy.wait_recv()
+
+        def body(index, carry):
+            at = pl.ds(pl.multiple_of(index * step, step), step)
+            self.mine[at, :] = (
+                self.grads[self.order[3], at, :].astype(jnp.float32)
+                + self.pair_in[3, at, :].astype(jnp.float32)
+                + self.near_in[0, at, :].astype(jnp.float32)
+                + self.near_in[1, at, :].astype(jnp.float32)
+            )
+            return carry
+
+        lax.fori_loop(0, 2 * self.half // step, body, 0)
+
+    def finish(self):
+        for copy in self.pair + [
+            self.far_x, self.far_y, self.x_low, self.y_high, self.y_low, self.x_high
+        ]:
+            copy.wait_send()
+
+
+def plane_boxes(block, wide):
+    low = jnp.bfloat16
+    return [
+        pltpu.VMEM((4, block, wide), low),
+        pltpu.VMEM((3, block, wide), low),
+        pltpu.VMEM((2, block // 2, wide), low),
+        pltpu.VMEM((2, block, wide), low),
+        pltpu.SemaphoreType.DMA((10,)),
+        pltpu.SemaphoreType.DMA((10,)),
+    ]
+
+
+def blocks(grads, size):
+    return grads.astype(jnp.bfloat16).reshape(size, grads.shape[0] // size, grads.shape[1])
+
+
+def mixed_kernel(
+    count, pieces, own, first, second, whole, mine_first, mine_second,
+    line_send, line_recv, local, *boxes
+):
+    meet(line_partners(lax.axis_index("tensor"), count) + plane_partners())
+    line = LineGather(own, whole, line_send, line_recv, count, pieces)
+    planes = [
+        PlaneScatter(first, mine_first, *boxes[:6]),
+        PlaneScatter(second, mine_second, *boxes[6:]),
+    ]
+    for piece in range(pieces):
+        line.start(0, piece)
+    for plane in planes:
+        plane.begin()
+    keep = pltpu.make_async_copy(own, whole.at[line.me], local.at[0])
+    keep.start()
+    planes[0].outward()
+    for piece in range(pieces):
+        line.arrive(0, piece)
+        line.start(1, piece)
+    planes[1].outward()
+    for piece in range(pieces):
+        line.arrive(1, piece)
+        line.start(2, piece)
+    planes[0].onward()
+    planes[1].onward()
+    for piece in range(pieces):
+        line.arrive(2, piece)
+    for plane in planes:
+        plane.take()
+    for plane in planes:
+        plane.finish()
+    line.finish()
+    keep.wait()
+
+
+def gather_and_scatter(own, first, second, count, size, pieces=2):
+    first, second = blocks(first, size), blocks(second, size)
+    whole, mine_first, mine_second = pl.pallas_call(
+        functools.partial(mixed_kernel, count, pieces),
+        out_shape=(
+            jax.ShapeDtypeStruct((count,) + own.shape, own.dtype),
+            jax.ShapeDtypeStruct(first.shape[1:], jnp.float32),
+            jax.ShapeDtypeStruct(second.shape[1:], jnp.float32),
+        ),
+        in_specs=[IN_VMEM] * 3,
+        out_specs=(IN_VMEM,) * 3,
+        scratch_shapes=[
+            pltpu.SemaphoreType.DMA((2, count - 1, pieces)),
+            pltpu.SemaphoreType.DMA((2, count - 1, pieces)),
+            pltpu.SemaphoreType.DMA((1,)),
+        ]
+        + plane_boxes(*first.shape[1:])
+        + plane_boxes(*second.shape[1:]),
+        compiler_params=pltpu.CompilerParams(
+            collective_id=9, has_side_effects=True, vmem_limit_bytes=60 * 1024 * 1024
+        ),
+        name="gather_and_scatter",
+    )(own, first, second)
+    return whole.reshape(count * own.shape[0], own.shape[1]), mine_first, mine_second
+
+
 def scatter_kernel(
-    count, size, pieces, parts, grads, small, total, mine, summed,
+    count, size, pieces, parts, first, second, small, total, mine_first, mine_second, summed,
     inbox, outbox, line_send, line_recv,
-    pair_in, held, far_in, near_in, send, recv,
-    small_dp, small_line, partial, small_send, small_recv,
+    small_dp, small_line, partial, small_send, small_recv, *boxes
 ):
     me, dp = lax.axis_index("tensor"), lax.axis_index("dp")
-    core, near_x, near_y = [dp + bit * (1 - 2 * ((dp // bit) % 2)) for bit in (1, 2, 4)]
-    far = near_x + 4 * (1 - 2 * ((dp // 4) % 2))
-    half = grads.shape[1] // 2
-    halves = [pl.ds(0, half), pl.ds(half, half)]
     meet(everyone(count, size))
     line = LineScatter(parts, inbox, outbox, line_send, line_recv, count, pieces)
+    planes = [
+        PlaneScatter(first, mine_first, *boxes[:6]),
+        PlaneScatter(second, mine_second, *boxes[6:]),
+    ]
     line.begin()
-    order = (far, near_x, near_y, dp)
-    pair = [
-        remote(
-            grads.at[dest + 1 - 2 * (dest % 2)], pair_in.at[k], send.at[k], recv.at[k],
-            {"dp": core},
-        )
-        for k, dest in enumerate(order)
-    ]
-    for copy in pair:
-        copy.start()
+    for plane in planes:
+        plane.begin()
     small_copies = [
         remote(small, small_dp.at[k - 1], small_send.at[k - 1], small_recv.at[k - 1],
                {"dp": lax.rem(dp + k, size)})
@@ -394,32 +553,8 @@
     ]
     for copy in small_copies:
         copy.start()
-
-    def ready(k, which):
-        rows = halves[which]
-        add_rows(held.at[k, rows], grads.at[order[k], rows], pair_in.at[k, rows], half)
-
-    def flow(slot, src, dst, target):
-        return remote(src, dst, send.at[slot], recv.at[slot], {"dp": target})
-
-    pair[0].wait_recv()
-    ready(0, 0)
-    far_x = flow(4, held.at[0, halves[0]], far_in.at[0], near_x)
-    far_x.start()
-    ready(0, 1)
-    far_y = flow(5, held.at[0, halves[1]], far_in.at[1], near_y)
-    far_y.start()
-    pair[1].wait_recv()
-    ready(1, 0)
-    x_low = flow(6, held.at[1, halves[0]], near_in.at[0, halves[0]], near_x)
-    x_low.start()
-    pair[2].wait_recv()
-    ready(2, 1)
-    y_high = flow(7, held.at[2, halves[1]], near_in.at[1, halves[1]], near_y)
-    y_high.start()
-    ready(1, 1)
-    ready(2, 0)
-    pair[3].wait_recv()
+    for plane in planes:
+        plane.outward()
     for copy in small_copies:
         copy.wait_recv()
     gathered = small[...]
@@ -435,14 +570,8 @@
         copy.start()
     for piece in range(pieces):
         line.relay(1, piece)
-    far_x.wait_recv()
-    add_rows(held.at[2, halves[0]], held.at[2, halves[0]], far_in.at[0], half)
-    y_low = flow(8, held.at[2, halves[0]], near_in.at[1, halves[0]], near_y)
-    y_low.start()
-    far_y.wait_recv()
-    add_rows(held.at[1, halves[1]], held.at[1, halves[1]], far_in.at[1], half)
-    x_high = flow(9, held.at[1, halves[1]], near_in.at[0, halves[1]], near_x)
-    x_high.start()
+    for plane in planes:
+        plane.onward()
     for time in range(2, count - 1):
         for piece in range(pieces):
             line.relay(time, piece)
@@ -453,64 +582,44 @@
         every = every + small_line[k]
     summed[0] = partial[...]
     summed[1] = every
+    for plane in planes:
+        plane.take()
     line.take(total)
-    step = 16
-    def last(rows_at, near_ready):
-        for copy in near_ready:
-            copy.wait_recv()
-        def body(index, carry):
-            at = pl.ds(pl.multiple_of(rows_at + index * step, step), step)
-            mine[at, :] = (
-                grads[dp, at, :].astype(jnp.float32)
-                + pair_in[3, at, :].astype(jnp.float32)
-                + near_in[0, at, :].astype(jnp.float32)
-                + near_in[1, at, :].astype(jnp.float32)
-            )
-            return carry
-        lax.fori_loop(0, half // step, body, 0)
-    last(0, (x_low, y_low))
-    last(half, (x_high, y_high))
-    for copy in pair + small_copies + tiny + [far_x, far_y, x_low, y_high, y_low, x_high]:
+    for copy in small_copies + tiny:
         copy.wait_send()
+    for plane in planes:
+        plane.finish()
     line.finish()
 
 
-def scatter_all(value, grads, small, count, size, pieces=2):
+def scatter_all(value, first, second, small, count, size, pieces=4):
     rows, cols = value.shape[0] // count, value.shape[1]
-    block, wide = grads.shape[0] // size, grads.shape[1]
-    low = jnp.bfloat16
+    first, second = blocks(first, size), blocks(second, size)
     return pl.pallas_call(
         functools.partial(scatter_kernel, count, size, pieces),
         out_shape=(
             jax.ShapeDtypeStruct((rows, cols), jnp.float32),
-            jax.ShapeDtypeStruct((block, wide), jnp.float32),
+            jax.ShapeDtypeStruct(first.shape[1:], jnp.float32),
+            jax.ShapeDtypeStruct(second.shape[1:], jnp.float32),
             jax.ShapeDtypeStruct((2,) + small.shape, jnp.float32),
         ),
-        in_specs=[IN_VMEM] * 3,
-        out_specs=(IN_VMEM,) * 3,
+        in_specs=[IN_VMEM] * 4,
+        out_specs=(IN_VMEM,) * 4,
         scratch_shapes=line_boxes(count, rows, cols, pieces)
         + [
-            pltpu.VMEM((4, block, wide), low),
-            pltpu.VMEM((3, block, wide), low),
-            pltpu.VMEM((2, block // 2, wide), low),
-            pltpu.VMEM((2, block, wide), low),
-            pltpu.SemaphoreType.DMA((10,)),
-            pltpu.SemaphoreType.DMA((10,)),
             pltpu.VMEM((size - 1,) + small.shape, jnp.float32),
             pltpu.VMEM((count - 1,) + small.shape, jnp.float32),
             pltpu.VMEM(small.shape, jnp.float32),
             pltpu.SemaphoreType.DMA((size + count - 2,)),
             pltpu.SemaphoreType.DMA((size + count - 2,)),
-        ],
+        ]
+        + plane_boxes(*first.shape[1:])
+        + plane_boxes(*second.shape[1:]),
         compiler_params=pltpu.CompilerParams(
-            collective_id=2, has_side_effects=True, vmem_limit_bytes=62 * 1024 * 1024
+            collective_id=2, has_side_effects=True, vmem_limit_bytes=60 * 1024 * 1024
         ),
         name="scatter_all",
-    )(
-        value.astype(low).reshape(count, rows, cols),
-        grads.astype(low).reshape(size, block, wide),
-        small,
-    )
+    )(value.astype(jnp.bfloat16).reshape(count, rows, cols), first, second, small)
 
 
 def unit_rows(value):
@@ -738,14 +847,20 @@
     gate_scale_grad = jnp.sum(g_gate * gate_sum, axis=0)
     g_up_low = (g_up * up_scale).astype(jnp.bfloat16)
     g_gate_low = (g_gate * gate_scale).astype(jnp.bfloat16)
-    up_grad = contract_rows(mid_whole, g_up_low)
-    gate_grad = contract_rows(mid_whole, g_gate_low)
+    both_grad = contract_rows(mid_whole, jnp.concatenate([g_up_low, g_gate_low], axis=1))
     g_mid_part = contract_cols(g_up_low, up_w) + contract_cols(g_gate_low, gate_w)
     g_mid = (1.0 - alpha_mlp) * g_second + line_scatter(g_mid_part, count, 8)
     g_first = unit_back(g_mid, mid, mid_norm)
     g_alpha_attn = jnp.sum((attn_unit - residual) * g_first, axis=0)
     g_attn_low = unit_back(alpha_attn * g_first, attn_unit, attn_norm).astype(jnp.bfloat16)
-    g_attn_whole = line_gather(g_attn_low, count, 6)
+    if size == 8:
+        g_attn_whole, both_grad, down_grad = gather_and_scatter(
+            g_attn_low, both_grad, down_grad, count, size
+        )
+    else:
+        g_attn_whole = line_gather(g_attn_low, count, 6)
+        both_grad, down_grad = scatter_low(both_grad, "dp"), scatter_low(down_grad, "dp")
+    up_grad, gate_grad = jnp.split(both_grad, 2, axis=1)
     out_grad = contract_rows(g_attn_whole, attended_low)
     g_attended_low = jnp.dot(g_attn_whole, out_w, preferred_element_type=jnp.float32).astype(
         jnp.bfloat16
@@ -763,34 +878,29 @@
         head_back(g_key * qk_scale, k_unit, k_norm, member), cosine, sine, first_half
     ).astype(jnp.bfloat16)
     g_value_low = g_value3.reshape(length, width).astype(jnp.bfloat16)
-    query_grad = contract_rows(whole, g_q_raw_low)
-    key_grad = contract_rows(whole, g_k_raw_low)
-    value_grad = contract_rows(whole, g_value_low)
+    triple_grad = contract_rows(
+        whole, jnp.concatenate([g_q_raw_low, g_k_raw_low, g_value_low], axis=1)
+    )
     g_tok_part = (
         contract_cols(g_q_raw_low, query_w)
         + contract_cols(g_k_raw_low, key_w)
         + contract_cols(g_value_low, value_w)
-    )
-    grads = jnp.concatenate(
-        [query_grad, key_grad, value_grad, out_grad, up_grad, gate_grad, down_grad], axis=1
     )
     model = g_alpha_attn.shape[0]
     vectors = (g_alpha_attn, g_alpha_mlp, up_scale_grad, gate_scale_grad, qk_grad)
     packed = jnp.concatenate(vectors)
     packed = jnp.pad(packed, (0, 8 * model - packed.shape[0])).reshape(8, model)
     if size == 8:
-        g_tokens, mine, sums = scatter_all(g_tok_part, grads, packed, count, size)
+        g_tokens, triple_grad, out_grad, sums = scatter_all(
+            g_tok_part, triple_grad, out_grad, packed, count, size
+        )
     else:
         g_tokens = line_scatter(g_tok_part, count, 2)
-        mine = scatter_low(grads, "dp")
+        triple_grad, out_grad = scatter_low(triple_grad, "dp"), scatter_low(out_grad, "dp")
         within = lax.psum(packed, "dp")
         sums = jnp.stack([within, lax.psum(within, "tensor")])
     tokens_grad = (1.0 - alpha_attn) * g_first + g_tokens
-    query_grad, key_grad, value_grad, out_grad, up_grad, gate_grad, down_grad = jnp.split(
-        mine,
-        (heads, 2 * heads, 3 * heads, 4 * heads, 4 * heads + units, 4 * heads + 2 * units),
-        axis=1,
-    )
+    query_grad, key_grad, value_grad = jnp.split(triple_grad, 3, axis=1)
     g_alpha_attn, g_alpha_mlp = sums[1, 0], sums[1, 1]
     flat = sums[0].reshape(8 * model)[2 * model :]
     up_scale_grad, gate_scale_grad = flat[:units], flat[units : 2 * units]

time: 681 us -> 621 us (0.912)
  local copies, waits for them, and re-layouts: 59.5 us -> 24.6 us
  matrix products: 157 us -> 142 us
  Pallas kernels: 411 us -> 404 us
    pallas_call x0 -> x1, Pallas kernels: none -> 53.7 us  [gather_and_scatter(): pl.pallas_call(functools.partial(mixed_kernel, count, pieces), out_shape=...]
    pallas_call x3 -> x2, Pallas kernels: 143 us -> 96.2 us  [line_gather(): pl.pallas_call(functools.partial(line_gather_kernel, count, pieces), out_...]
    concatenate x1 -> x0, local copies, waits for them, and re-layouts: 20.2 us -> none  [on_device(): jnp.concatenate([query_grad, key_grad, value_grad, out_grad, up_grad, gat...]
    dot_general x4 -> x0, local copies, waits for them, and re-layouts: 18.5 us -> none  [contract_rows(): lax.dot_general(left, right, (((0,), (0,)), ((), ())), preferred_element_...]
    pallas_call x1, Pallas kernels: 69.4 us -> 55.3 us  [scatter_all(): pl.pallas_call(functools.partial(scatter_kernel, count, size, pieces), ou...]
    dot_general x7 -> x4, matrix products: 30.1 us -> 22.5 us  [contract_rows(): lax.dot_general(left, right, (((0,), (0,)), ((), ())), preferred_element_...]
where the time goes in v3:
time: 621 us; the launch traced here: 616 us
  Pallas kernels  404 us (65%)
  matrix products  142 us (23%)
  other arithmetic  43.1 us (7%)
  local copies, waits for them, and re-layouts  24.6 us (4%)
    pallas_call x3, Pallas kernels, line_scatter(): pl.pallas_call(functools.partial(line_scatter_kernel, count, pieces), out...  136 us
    pallas_call x2, Pallas kernels, line_gather(): pl.pallas_call(functools.partial(line_gather_kernel, count, pieces), out_...  96.2 us
    pallas_call x1, Pallas kernels, gather_all(): pl.pallas_call(functools.partial(gather_kernel, count, pieces), out_shape...  63.3 us
    pallas_call x1, Pallas kernels, scatter_all(): pl.pallas_call(functools.partial(scatter_kernel, count, size, pieces), ou...  55.3 us
    pallas_call x1, Pallas kernels, gather_and_scatter(): pl.pallas_call(functools.partial(mixed_kernel, count, pieces), out_shape=...  53.7 us
    dot_general x7, matrix products, contract_cols(): lax.dot_general(left, right, (((1,), (1,)), ((), ())), preferred_element_...  31.2 us
    dot_general x4, matrix products, contract_rows(): lax.dot_general(left, right, (((0,), (0,)), ((), ())), preferred_element_...  22.5 us

profile of v3, /device:TPU:0, one launch (start us, length us, event | category | flops | bytes accessed | tf_op | source)
XLA Modules:
  0.0 615.8 jit_solution(12726850025064693674)
XLA Ops:
  3.2 3.9 concatenate.61.shard
  7.1 63.3 %gather_all.1 = (bf16[4,256,1280]{2,1,0:T(8,128)(2,1)}, bf16[8,160,5120]{2,1,0:T(8,128)(2,1)}) custom-call(bf16[256,1280]{1,0:T(8,128)(2,1)} %tokens.1, bf16[160,5120]{1,0:T(8,128)(2,1)} %concatenate.61.shard), custom_call_target="tpu_custom_call" | custom-call | tf_op jit(solution)/shard_map/gather_all/pallas_call | solution.py:184
  70.5 3.2 convolution_convert_fusion.7
  79.8 6.6 %fusion.38 = (f32[1024,320]{0,1:T(8,128)S(1)}, f32[1024,320]{0,1:T(8,128)S(1)}) fusion(f32[1024,32]{0,1:T(8,128)S(1)} %get-tuple-element.130, f32[1024,288]{0,1:T(8,128)S(1)} %get-tuple-element.132, f32[1024,288]{0,1:T(8,128)S(1)} %get-tuple-element.131, f32[1024,32]{0,1:T(8,128)S(1)} %get-tuple-element.129, f32[1024,320]{0,1:T(8,128)S(1)} %fusion.88, ...), kind=kLoop, calls=%fused_computation.76 | loop fusion | flops 4915200 | bytes 10487360 | tf_op jit(solution)/shard_map/add | solution.py:668
  100.3 3.4 exponential_reduce_fusion
  107.1 4.6 convolution_convert_fusion.3
  111.7 47.7 %line_scatter_4.1 = f32[256,1280]{1,0:T(8,128)} custom-call(bf16[4,256,1280]{2,1,0:T(8,128)(2,1)} %bitcast.121), custom_call_target="tpu_custom_call" | custom-call | tf_op jit(solution)/shard_map/line_scatter_4/pallas_call | solution.py:355
  163.7 49.4 %line_gather_3.1 = bf16[4,256,1280]{2,1,0:T(8,128)(2,1)} custom-call(bf16[256,1280]{1,0:T(8,128)(2,1)} %multiply_convert_fusion.10.own), custom_call_target="tpu_custom_call" | custom-call | tf_op jit(solution)/shard_map/line_gather_3/pallas_call | solution.py:327
  213.2 6.4 %fusion.11 = f32[1024,1280]{1,0:T(8,128)S(1)} fusion(bf16[1024,1280]{1,0:T(8,128)(2,1)} %bitcast.115, bf16[1280,5120]{1,0:T(8,128)(2,1)} %bitcast.135), kind=kOutput, calls=%fused_computation.35 | convolution fusion | flops 3355443200 | bytes 11141120 | tf_op jit(solution)/shard_map/dot_general | solution.py:829
  219.6 9.5 %multiply_convert_fusion.4 = (bf16[1024,1280]{1,0:T(8,128)(2,1)S(1)}, f32[1024,1280]{1,0:T(8,128)}) fusion(f32[1280]{0:T(1024)S(1)} %copy-done.69, f32[1024,1280]{1,0:T(8,128)S(1)} %fusion.11, f32[1280]{0:T(1024)S(1)} %copy-done.63, bf16[1024,1280]{1,0:T(8,128)(2,1)S(1)} %bitcast.116, bf16[1280,5120]{1,0:T(8,128)(2,1)} %bitcast.136), kind=kOutput, calls=%fused_computation.21 | convolution fusion | flops 3365928960 | bytes 19015680 | tf_op jit(solution)/shard_map/dot_general | solution.py:828
  229.2 7.7 %convolution_convert_fusion.2 = bf16[1024,1280]{1,0:T(8,128)(2,1)} fusion(bf16[1024,1280]{1,0:T(8,128)(2,1)S(1)} %get-tuple-element.157, bf16[1280,5120]{1,0:T(8,128)(2,1)} %bitcast.137), kind=kOutput, calls=%fused_computation.28 | convolution fusion | flops 3356753920 | bytes 8519680 | tf_op jit(solution)/shard_map/dot_general | solution.py:641
  236.9 44.7 %line_scatter_7.1 = f32[256,1280]{1,0:T(8,128)} custom-call(bf16[4,256,1280]{2,1,0:T(8,128)(2,1)} %bitcast.122), custom_call_target="tpu_custom_call" | custom-call | tf_op jit(solution)/shard_map/line_scatter_7/pallas_call | solution.py:355
  288.1 46.8 %line_gather_5.1 = bf16[4,256,1280]{2,1,0:T(8,128)(2,1)} custom-call(bf16[256,1280]{1,0:T(8,128)(2,1)} %multiply_convert_fusion.6.own), custom_call_target="tpu_custom_call" | custom-call | tf_op jit(solution)/shard_map/line_gather_5/pallas_call | solution.py:327
  335.0 11.1 %multiply_reduce_fusion.1 = (f32[1280]{0:T(1024)S(1)}, f32[1280]{0:T(1024)S(1)}, f32[1024,1280]{1,0:T(8,128)S(1)}, bf16[1024,1280]{1,0:T(8,128)(2,1)S(1)}) fusion(f32[1024,1280]{1,0:T(8,128)} %copy-done.70, f32[1024,1280]{1,0:T(8,128)} %get-tuple-element.158, f32[1280]{0:T(1024)S(1)} %copy-done.63, f32[1280]{0:T(1024)S(1)} %copy-done.69, ...), kind=kOutput, calls=%fused_computation.12 | convolution fusion | flops 3380344320 | bytes 24268800 | tf_op jit(solution)/shard_map/dot_general | solution.py:843
  346.1 5.1 convolution_convert_fusion.1
  352.9 9.3 %convolution_convert_fusion = bf16[1280,2560]{1,0:T(8,128)(2,1)} fusion(bf16[1024,1280]{1,0:T(8,128)(2,1)S(1)} %bitcast.117, bf16[1024,1280]{1,0:T(8,128)(2,1)S(1)} %multiply_convert_fusion.2, bf16[1024,1280]{1,0:T(8,128)(2,1)S(1)} %get-tuple-element.117), kind=kOutput, calls=%fused_computation | convolution fusion | flops 6724648960 | bytes 14417920 | tf_op jit(solution)/shard_map/dot_general | solution.py:635
  362.2 3.6 fusion.13
  365.8 5.1 add_convert_fusion.1
  370.9 43.2 %line_scatter_8.1 = f32[256,1280]{1,0:T(8,128)} custom-call(bf16[4,256,1280]{2,1,0:T(8,128)(2,1)} %bitcast.120), custom_call_target="tpu_custom_call" | custom-call | tf_op jit(solution)/shard_map/line_scatter_8/pallas_call | solution.py:355
  419.5 53.7 %gather_and_scatter.1 = (bf16[4,256,1280]{2,1,0:T(8,128)(2,1)}, f32[160,2560]{1,0:T(8,128)}, f32[160,1280]{1,0:T(8,128)}) custom-call(bf16[256,1280]{1,0:T(8,128)(2,1)} %multiply_convert_fusion.5.own, bf16[8,160,2560]{2,1,0:T(8,128)(2,1)} %bitcast.106, bf16[8,160,1280]{2,1,0:T(8,128)(2,1)} %bitcast.110), custom_call_target="tpu_custom_call" | custom-call | tf_op jit(solution)/shard_map/gather_and_scatter/pallas_call | solution.py:510
  480.2 4.1 convolution_bitcast_fusion.1
  484.3 6.6 %fusion.30 = bf16[1024,5,64]{0,2,1:T(8,128)(2,1)} fusion(bf16[512,5,64]{0,2,1:T(8,128)(2,1)S(1)} %bitcast.129, f32[512,5,64]{0,2,1:T(8,128)S(1)} %convolution_bitcast_fusion.1, f32[5,512,1024]{2,1,0:T(8,128)} %copy-done, f32[5,512]{1,0:T(8,128)S(1)} %log_add_fusion, pred[512,1024]{1,0:T(8,128)(4,1)S(1)} %iota_compare_fusion), kind=kOutput, calls=%fused_computation.64 | convolution fusion | flops 346685440 | bytes 12658688 | tf_op jit(solution)/shard_map/hqk,qhd->khd/dot_general | solution.py:758
  500.7 3.8 multiply_reduce_fusion
  504.6 3.0 multiply_convert_fusion
  513.7 3.1 fusion.76
  520.1 7.2 %fusion.53 = (f32[1024,320]{0,1:T(8,128)S(1)}, f32[1024,320]{0,1:T(8,128)S(1)}, f32[1024,320]{0,1:T(8,128)S(1)}) fusion(f32[320]{0:T(512)S(1)} %copy-done.60, f32[1024,320]{0,1:T(8,128)S(1)} %fusion.27, f32[1024,320]{0,1:T(8,128)S(1)} %copy-done.20, f32[1024,320]{0,1:T(8,128)S(1)} %copy-done.8, f32[1024,5]{1,0:T(8,128)S(1)} %fusion.79, ...), kind=kOutput, calls=%fused_computation.116 | convolution fusion | flops 21957760 | bytes 9200960 | tf_op jit(solution)/shard_map/dot_general | solution.py:695
  528.3 5.6 fusion.42
  533.9 5.3 convolution_convert_fusion.4
  539.2 4.5 copy.38
  546.4 3.0 fusion.86
  549.5 4.3 add_convert_fusion
  553.8 55.3 %scatter_all.1 = (f32[256,1280]{1,0:T(8,128)}, f32[160,960]{1,0:T(8,128)}, f32[160,320]{1,0:T(8,128)}, f32[2,8,1280]{2,1,0:T(8,128)}) custom-call(bf16[4,256,1280]{2,1,0:T(8,128)(2,1)} %bitcast.102, bf16[8,160,960]{2,1,0:T(8,128)(2,1)} %bitcast.103, bf16[8,160,320]{2,1,0:T(8,128)(2,1)} %bitcast.107, f32[8,1280]{1,0:T(8,128)} %reshape.365.small), custom_call_target="tpu_custom_call" | custom-call | tf_op jit(solution)/shard_map/scatter_all/pallas_call | solution.py:598
  (252 shorter events, 79.5 us)
Async XLA Ops:
  0.7 89.7 %copy-start.57 = (pred[320]{0:T(512)(128)(4,1)}, pred[320]{0:T(512)(128)(4,1)S(1)}, u32[]{:S(2)}) copy-start(pred[320]{0:T(512)(128)(4,1)S(1)} %fusion.137) | copy-start | bytes 964
  0.7 79.1 %copy-start.64 = (pred[320]{0:T(512)(128)(4,1)}, pred[320]{0:T(512)(128)(4,1)S(1)}, u32[]{:S(2)}) copy-start(pred[320]{0:T(512)(128)(4,1)S(1)} %fusion.135) | copy-start | bytes 964
  0.7 79.1 %copy-start.59 = (f32[320]{0:T(512)}, f32[320]{0:T(512)S(1)}, u32[]{:S(2)}) copy-start(f32[320]{0:T(512)S(1)} %fusion.131) | copy-start | bytes 3844
  0.7 89.6 %copy-start.47 = (s32[320]{0:T(512)}, s32[320]{0:T(512)S(1)}, u32[]{:S(2)}) copy-start(s32[320]{0:T(512)S(1)} %get-tuple-element.168) | copy-start | bytes 3844
  0.8 89.6 %copy-start.49 = (s32[320]{0:T(512)}, s32[320]{0:T(512)S(1)}, u32[]{:S(2)}) copy-start(s32[320]{0:T(512)S(1)} %get-tuple-element.169) | copy-start | bytes 3844
  2.8 477.4 %copy-start.16 = (pred[512,512]{0,1:T(8,128)(4,1)}, pred[512,512]{0,1:T(8,128)(4,1)S(1)}, u32[]{:S(2)}) copy-start(pred[512,512]{0,1:T(8,128)(4,1)S(1)} %iota_compare_fusion.1) | copy-start | bytes 786436
  73.7 30.0 %copy-start.31 = (bf16[1024,320]{0,1:T(8,128)(2,1)}, bf16[1024,320]{0,1:T(8,128)(2,1)S(1)}, u32[]{:S(2)}) copy-start(bf16[1024,320]{0,1:T(8,128)(2,1)S(1)} %convolution_convert_fusion.7) | copy-start | bytes 1966084
  73.7 22.0 %copy-start.35 = (bf16[512,320]{0,1:T(8,128)(2,1)}, bf16[512,320]{0,1:T(8,128)(2,1)S(1)}, u32[]{:S(2)}) copy-start(bf16[512,320]{0,1:T(8,128)(2,1)S(1)} %slice.245) | copy-start | bytes 983044
  98.3 8.8 %copy-start.42 = (bf16[5,64,512]{2,1,0:T(8,128)(2,1)}, bf16[5,64,512]{2,1,0:T(8,128)(2,1)S(1)}, u32[]{:S(2)}) copy-start(bf16[5,64,512]{2,1,0:T(8,128)(2,1)S(1)} %convolution_convert_fusion.9) | copy-start | bytes 983044
  111.7 49.2 %copy-start.18 = (bf16[256,1280]{1,0:T(8,128)(2,1)S(1)}, bf16[256,1280]{1,0:T(8,128)(2,1)}, u32[]{:S(2)}) copy-start(bf16[256,1280]{1,0:T(8,128)(2,1)} %tokens.1) | copy-start | bytes 1966084
  111.7 49.2 %copy-start.52 = (f32[1280]{0:T(1024)S(1)}, f32[1280]{0:T(1024)}, u32[]{:S(2)}) copy-start(f32[1280]{0:T(1024)} %param.37) | copy-start | bytes 15364
  213.1 6.5 %copy-start.27 = (bf16[4,256,1280]{2,1,0:T(8,128)(2,1)S(1)}, bf16[4,256,1280]{2,1,0:T(8,128)(2,1)}, u32[]{:S(2)}) copy-start(bf16[4,256,1280]{2,1,0:T(8,128)(2,1)} %line_gather_3.1) | copy-start | bytes 7864324
  213.1 6.5 %copy-start.63 = (f32[1280]{0:T(1024)S(1)}, f32[1280]{0:T(1024)}, u32[]{:S(2)}) copy-start(f32[1280]{0:T(1024)} %param.36) | copy-start | bytes 15364
  219.6 9.5 %copy-start.70 = (f32[1024,1280]{1,0:T(8,128)}, f32[1024,1280]{1,0:T(8,128)S(1)}, u32[]{:S(2)}) copy-start(f32[1024,1280]{1,0:T(8,128)S(1)} %fusion.11) | copy-start | bytes 15728644
  229.2 7.7 %copy-start.71 = (bf16[1024,1280]{1,0:T(8,128)(2,1)}, bf16[1024,1280]{1,0:T(8,128)(2,1)S(1)}, u32[]{:S(2)}) copy-start(bf16[1024,1280]{1,0:T(8,128)(2,1)S(1)} %get-tuple-element.157) | copy-start | bytes 7864324
  236.9 46.2 %copy-start.51 = (f32[1280]{0:T(1024)S(1)}, f32[1280]{0:T(1024)}, u32[]{:S(2)}) copy-start(f32[1280]{0:T(1024)} %param.38) | copy-start | bytes 15364
  334.9 11.1 %copy-start.29 = (bf16[4,256,1280]{2,1,0:T(8,128)(2,1)S(1)}, bf16[4,256,1280]{2,1,0:T(8,128)(2,1)}, u32[]{:S(2)}) copy-start(bf16[4,256,1280]{2,1,0:T(8,128)(2,1)} %line_gather_5.1) | copy-start | bytes 7864324
  334.9 11.1 %copy-start.72 = (bf16[1024,1280]{1,0:T(8,128)(2,1)S(1)}, bf16[1024,1280]{1,0:T(8,128)(2,1)}, u32[]{:S(2)}) copy-start(bf16[1024,1280]{1,0:T(8,128)(2,1)} %copy-done.71) | copy-start | bytes 7864324
  351.2 11.0 %slice-start.5 = ((s8[13107200]{0:T(1024)(128)(4,1)}), s8[4194304]{0:T(1024)(128)(4,1)S(1)}, s32[]{:S(2)}) async-start(s8[13107200]{0:T(1024)(128)(4,1)} %bitcast.143), calls=%async_computation.5 | async-start | bytes 8388608
  352.9 9.3 %slice-start.6 = ((s8[13107200]{0:T(1024)(128)(4,1)}), s8[4194304]{0:T(1024)(128)(4,1)S(1)}, s32[]{:S(2)}) async-start(s8[13107200]{0:T(1024)(128)(4,1)} %bitcast.143), calls=%async_computation.6 | async-start | bytes 8388608
  352.9 9.3 %slice-start.7 = ((s8[13107200]{0:T(1024)(128)(4,1)}), s8[4194304]{0:T(1024)(128)(4,1)S(1)}, s32[]{:S(2)}) async-start(s8[13107200]{0:T(1024)(128)(4,1)} %bitcast.143), calls=%async_computation.7 | async-start | bytes 8388608
  352.9 9.3 %slice-start.8 = ((s8[13107200]{0:T(1024)(128)(4,1)}), s8[524288]{0:T(1024)(128)(4,1)S(1)}, s32[]{:S(2)}) async-start(s8[13107200]{0:T(1024)(128)(4,1)} %bitcast.143), calls=%async_computation.8 | async-start | bytes 1048576
  417.3 55.9 %copy-start.61 = (f32[5440]{0:T(1024)}, f32[5440]{0:T(1024)S(1)}, u32[]{:S(2)}) copy-start(f32[5440]{0:T(1024)S(1)} %constant_dynamic-update-slice_fusion.1) | copy-start | bytes 65284
  419.5 53.7 %copy-start.43 = (bf16[5,64,512]{2,1,0:T(8,128)(2,1)S(1)}, bf16[5,64,512]{2,1,0:T(8,128)(2,1)}, u32[]{:S(2)}) copy-start(bf16[5,64,512]{2,1,0:T(8,128)(2,1)} %copy-done.42) | copy-start | bytes 983044
  419.5 53.7 %copy-start.45 = (bf16[5,64,512]{2,1,0:T(8,128)(2,1)S(1)}, bf16[5,64,512]{2,1,0:T(8,128)(2,1)}, u32[]{:S(2)}) copy-start(bf16[5,64,512]{2,1,0:T(8,128)(2,1)} %copy-done.44) | copy-start | bytes 983044
  480.2 12.0 %slice-start.3 = ((s8[5242880]{0:T(1024)(128)(4,1)}), s8[4194304]{0:T(1024)(128)(4,1)S(1)}, s32[]{:S(2)}) async-start(s8[5242880]{0:T(1024)(128)(4,1)} %bitcast.94), calls=%async_computation.3 | async-start | bytes 8388608
  484.3 6.7 %copy-start.30 = (f32[160,2560]{1,0:T(8,128)S(1)}, f32[160,2560]{1,0:T(8,128)}, u32[]{:S(2)}) copy-start(f32[160,2560]{1,0:T(8,128)} %get-tuple-element.93) | copy-start | bytes 4915204
  484.3 7.9 %slice-start.4 = ((s8[5242880]{0:T(1024)(128)(4,1)}), s8[1048576]{0:T(1024)(128)(4,1)S(1)}, s32[]{:S(2)}) async-start(s8[5242880]{0:T(1024)(128)(4,1)} %bitcast.94), calls=%async_computation.4 | async-start | bytes 2097152
  492.5 7.7 %slice-start = ((s8[10485760]{0:T(1024)(128)(4,1)}), s8[4194304]{0:T(1024)(128)(4,1)S(1)}, s32[]{:S(2)}) async-start(s8[10485760]{0:T(1024)(128)(4,1)} %bitcast.92), calls=%async_computation | async-start | bytes 8388608
  492.5 7.7 %slice-start.1 = ((s8[10485760]{0:T(1024)(128)(4,1)}), s8[4194304]{0:T(1024)(128)(4,1)S(1)}, s32[]{:S(2)}) async-start(s8[10485760]{0:T(1024)(128)(4,1)} %bitcast.92), calls=%async_computation.1 | async-start | bytes 8388608
  553.8 55.3 %copy-start.13 = (f32[256,1280]{1,0:T(8,128)S(1)}, f32[256,1280]{1,0:T(8,128)}, u32[]{:S(2)}) copy-start(f32[256,1280]{1,0:T(8,128)} %copy-done.12) | copy-start | bytes 3932164
  553.8 55.4 %copy-start.56 = (f32[1280]{0:T(1024)S(1)}, f32[1280]{0:T(1024)}, u32[]{:S(2)}) copy-start(f32[1280]{0:T(1024)} %broadcast_subtract_fusion.1) | copy-start | bytes 15364
  (50 other events, 139.1 us)
